TPU v7x, 16 devices: a 4x2x1 block of a 4x4x8 slice. The times are simulated.
16 devices in a mesh: rep: 4 (over y, z, core), dp: 4 (over x).
Axes of the slice: x: 4, y: 2, z: 1, core: 2. Of those that a mesh axis runs over, the one named last changes fastest.
The devices are a block of a 4x4x8 slice.
Arguments:
- x: bfloat16 [16, 4096, 896], P(('rep', 'dp')), parts along dimension 0
- dy: bfloat16 [16, 4096, 896], P(('rep', 'dp')), parts along dimension 0
- w_gate: bfloat16 [2, 896, 2304], P(None, 'dp')
- w_up: bfloat16 [2, 896, 2304], P(None, 'dp')
- w_down: bfloat16 [2, 2304, 896], P(None, 'dp')
Outputs:
- output 1: bfloat16 [16, 4096, 896], P(('rep', 'dp')), parts along dimension 0
- output 2: bfloat16 [8, 896, 2304], P('rep', 'dp'), parts along dimension 0
- output 3: bfloat16 [8, 896, 2304], P('rep', 'dp'), parts along dimension 0
- output 4: bfloat16 [8, 2304, 896], P('rep', 'dp'), parts along dimension 0
There are 4 independent parts. A program takes and returns all parts, laid end to end along the dimension named above; an argument that names none is the same for every part.
All inputs are finite; a program needn't handle non-finite values.
Results may differ from a plain program's by a relative error of at most 0.018.
Values are sent between devices in bfloat16 or wider.
A program may use at most 768 MiB of HBM per device.

v0:
```python
import jax
import jax.numpy as jnp
from jax import lax

NAMES = ("w_gate", "w_up", "w_down")


def matmul(a, w):
    return jnp.dot(a, w, preferred_element_type=jnp.float32).astype(jnp.bfloat16)


def normed(h):
    wide = h.astype(jnp.float32)
    scale = lax.rsqrt(jnp.mean(wide**2, -1, keepdims=True) + 1e-6)
    return (wide * scale).astype(jnp.bfloat16)


def layer(h, w):
    a = normed(h)
    gate = jnp.dot(a, w["w_gate"], preferred_element_type=jnp.float32)
    up = jnp.dot(a, w["w_up"], preferred_element_type=jnp.float32)
    return h + matmul((jax.nn.silu(gate) * up).astype(jnp.bfloat16), w["w_down"])


def stack(weights, h):
    for number in range(weights["w_gate"].shape[0]):
        h = layer(h, {name: w[number] for name, w in weights.items()})
    return h


def solution(mesh):
    groups = mesh.shape["rep"]

    def step(x, dy, *weights):
        shape = x.shape
        x, dy = (t.reshape(groups, -1, *t.shape[1:]) for t in (x, dy))

        def of_a_group(x, dy):
            _, back = jax.vjp(stack, dict(zip(NAMES, weights, strict=True)), x)
            by_weights, by_x = back(dy)
            return (by_x, *(by_weights[name] for name in NAMES))

        by_x, *by_weights = jax.vmap(of_a_group)(x, dy)
        return (by_x.reshape(shape), *(t.reshape(-1, *t.shape[2:]) for t in by_weights))

    return step
```

profile of v0, /device:TPU:112, one launch (start us, length us, event | category | flops | bytes accessed | tf_op | source)
XLA Modules:
  0.0 913.8 jit_solution(4818369261527641478)
XLA Ops:
  56.8 26.8 %fusion.97 = f32[4096,2304]{1,0:T(8,128)} fusion(bf16[1,896,2304]{2,1,0:T(8,128)(2,1)} %all-gather.30.cloned.1.call-done, bf16[1,4096,896]{2,1,0:T(8,128)(2,1)} %param.1, f32[4096]{0:T(1024)S(1)} %get-tuple-element.13), kind=kOutput, calls=%fused_computation.99 | convolution fusion | flops 16922443776 | bytes 49233920 | tf_op jit(solution)/vmap(jvp())/dot_general | solution.py:20
  83.6 19.1 %all-gather.32.cloned.1.call-done = bf16[1,896,2304]{2,1,0:T(8,128)(2,1)} async-done(((bf16[1,224,2304]{2,1,0:T(8,128)(2,1)}), bf16[1,896,2304]{2,1,0:T(8,128)(2,1)}) %all-gather.32.cloned.1.call-update) | async-done | bytes 4128784 | tf_op jit(solution)/vmap(jvp())/squeeze | solution.py:27
  102.7 26.7 %fusion.93 = f32[4096,2304]{1,0:T(8,128)} fusion(bf16[1,896,2304]{2,1,0:T(8,128)(2,1)} %all-gather.32.cloned.1.call-done, bf16[1,4096,896]{2,1,0:T(8,128)(2,1)} %param.1, f32[4096]{0:T(1024)S(1)} %get-tuple-element.13), kind=kOutput, calls=%fused_computation.95 | convolution fusion | flops 16922443776 | bytes 49233920 | tf_op jit(solution)/vmap(jvp())/dot_general | solution.py:21
  129.4 31.7 %fusion.26 = bf16[4096,2304]{1,0:T(8,128)(2,1)} fusion(f32[4096,2304]{1,0:T(8,128)} %fusion.93, f32[4096,2304]{1,0:T(8,128)} %fusion.97), kind=kLoop, calls=%fused_computation.45 | loop fusion | flops 56623104 | bytes 94371840
  161.1 24.7 %fusion.38 = (f32[4096]{0:T(1024)S(1)}, bf16[1,1,4096,896]{2,3,1,0:T(8,128)(2,1)}) fusion(bf16[4096,2304]{1,0:T(8,128)(2,1)} %fusion.26, bf16[1,2304,896]{2,1,0:T(8,128)(2,1)} %all-gather.34.cloned.1.call-done, bf16[1,4096,896]{1,2,0:T(8,128)(2,1)} %copy.1), kind=kOutput, calls=%fused_computation.60 | convolution fusion | flops 16929779712 | bytes 37699584 | tf_op jit(solution)/vmap(jvp())/dot_general | solution.py:9
  193.9 26.9 %fusion.82 = f32[4096,2304]{1,0:T(8,128)} fusion(bf16[1,1,4096,896]{2,3,1,0:T(8,128)(2,1)} %get-tuple-element.15, f32[4096]{0:T(1024)S(1)} %bitcast.261, bf16[1,896,2304]{2,1,0:T(8,128)(2,1)} %all-gather.36.cloned.1.call-done), kind=kOutput, calls=%fused_computation.85 | convolution fusion | flops 16922443776 | bytes 49233920 | tf_op jit(solution)/vmap(jvp())/dot_general | solution.py:20
  220.8 18.9 %all-gather.40.cloned.1.call-done = bf16[1,896,2304]{2,1,0:T(8,128)(2,1)} async-done(((bf16[1,224,2304]{2,1,0:T(8,128)(2,1)}), bf16[1,896,2304]{2,1,0:T(8,128)(2,1)}) %all-gather.40.cloned.1.call-update) | async-done | bytes 4128784 | tf_op jit(solution)/vmap(jvp())/squeeze | solution.py:27
  239.7 27.2 %fusion.80 = f32[4096,2304]{1,0:T(8,128)} fusion(bf16[1,1,4096,896]{2,3,1,0:T(8,128)(2,1)} %get-tuple-element.15, f32[4096]{0:T(1024)S(1)} %bitcast.262, bf16[1,896,2304]{2,1,0:T(8,128)(2,1)} %all-gather.40.cloned.1.call-done), kind=kOutput, calls=%fused_computation.84 | convolution fusion | flops 16922443776 | bytes 49233920 | tf_op jit(solution)/vmap(jvp())/dot_general | solution.py:21
  285.0 26.5 %fusion.24 = bf16[1,1,4096,2304]{3,2,1,0:T(8,128)(2,1)} fusion(bf16[1,4096,896]{2,1,0:T(8,128)(2,1)} %param, bf16[1,2304,896]{2,1,0:T(8,128)(2,1)} %all-gather.38.cloned.1.call-done), kind=kOutput, calls=%fused_computation.43 | convolution fusion | flops 16920870912 | bytes 30343168 | tf_op jit(solution)/vmap(transpose(jvp()))/dot_general | solution.py:9
  311.4 30.6 %fusion.4 = bf16[4096,2304]{1,0:T(8,128)(2,1)S(1)} fusion(f32[4096,2304]{1,0:T(8,128)} %fusion.82, f32[4096,2304]{1,0:T(8,128)} %fusion.80, bf16[1,1,4096,2304]{3,2,1,0:T(8,128)(2,1)} %fusion.24), kind=kLoop, calls=%fused_computation.10 | loop fusion | flops 113246208 | bytes 113246208
  348.5 19.1 %fusion.87 = bf16[4096,896]{0,1:T(8,128)(2,1)} fusion(bf16[4096,2304]{1,0:T(8,128)(2,1)S(1)} %fusion.4, bf16[1,896,2304]{2,1,0:T(8,128)(2,1)S(1)} %copy-done.10), kind=kOutput, calls=%fused_computation.89 | convolution fusion | flops 16911433728 | bytes 30343168 | tf_op jit(solution)/vmap(transpose(jvp()))/dot_general | solution.py:20
  367.6 35.0 %fusion.40 = (f32[4096]{0:T(1024)S(1)}, bf16[4096,896]{0,1:T(8,128)(2,1)}) fusion(bf16[1,1,4096,896]{2,3,1,0:T(8,128)(2,1)} %get-tuple-element.15, bf16[4096,896]{0,1:T(8,128)(2,1)} %fusion.87, bf16[1,896,2304]{2,1,0:T(8,128)(2,1)} %all-gather.40.cloned.1.call-done, bf16[1,1,4096,2304]{3,2,1,0:T(8,128)(2,1)} %fusion.24, f32[4096,2304]{1,0:T(8,128)} %fusion.82), kind=kOutput, calls=%fused_computation.62 | convolution fusion | flops 16990072832 | bytes 82788352 | tf_op jit(solution)/vmap(transpose(jvp()))/dot_general | solution.py:21
  415.4 24.8 %fusion.65 = f32[1,2304,896]{2,1,0:T(8,128)} fusion(bf16[4096,2304]{1,0:T(8,128)(2,1)} %fusion.26, bf16[1,1,4096,896]{2,3,1,0:T(8,128)(2,1)S(1)} %fusion.45), kind=kOutput, calls=%fused_computation.80 | convolution fusion | flops 16911433728 | bytes 34471936 | tf_op jit(solution)/vmap(transpose(jvp()))/dot_general | solution.py:9
  440.3 34.6 %fusion.68 = f32[1,2304,896]{2,1,0:T(8,128)} fusion(bf16[1,4096,896]{2,1,0:T(8,128)(2,1)} %param, f32[4096,2304]{1,0:T(8,128)} %fusion.80, f32[4096,2304]{1,0:T(8,128)} %fusion.82), kind=kOutput, calls=%fused_computation.82 | convolution fusion | flops 16968056832 | bytes 91095040 | tf_op jit(solution)/vmap(transpose(jvp()))/dot_general | solution.py:9
  475.0 27.4 %fusion.25 = bf16[1,1,4096,2304]{3,2,1,0:T(8,128)(2,1)} fusion(bf16[1,1,4096,896]{2,3,1,0:T(8,128)(2,1)} %copy-done, bf16[1,2304,896]{2,1,0:T(8,128)(2,1)} %all-gather.34.cloned.1.call-done), kind=kOutput, calls=%fused_computation.44 | convolution fusion | flops 16920870912 | bytes 30343168 | tf_op jit(solution)/vmap(transpose(jvp()))/dot_general | solution.py:9
  502.4 37.7 %fusion.7 = bf16[4096,2304]{1,0:T(8,128)(2,1)} fusion(f32[4096,2304]{1,0:T(8,128)} %fusion.97, f32[4096,2304]{1,0:T(8,128)} %fusion.93, bf16[1,1,4096,2304]{3,2,1,0:T(8,128)(2,1)} %fusion.25), kind=kLoop, calls=%fused_computation.13 | loop fusion | flops 113246208 | bytes 113246208
  540.2 28.8 %fusion.59 = f32[1,896,2304]{2,1,0:T(8,128)} fusion(bf16[1,1,4096,2304]{3,2,1,0:T(8,128)(2,1)} %fusion.24, f32[4096,2304]{1,0:T(8,128)} %fusion.82, bf16[1,1,4096,896]{2,3,1,0:T(8,128)(2,1)} %get-tuple-element.15, f32[4096]{0:T(1024)S(1)} %bitcast.264), kind=kOutput, calls=%fused_computation.78 | convolution fusion | flops 16979066880 | bytes 72237056 | tf_op jit(solution)/vmap(transpose(jvp()))/dot_general | solution.py:21
  569.1 22.9 %fusion.95 = bf16[4096,896]{0,1:T(8,128)(2,1)} fusion(bf16[4096,2304]{1,0:T(8,128)(2,1)} %fusion.7, bf16[1,896,2304]{2,1,0:T(8,128)(2,1)} %all-gather.30.cloned.1.call-done), kind=kOutput, calls=%fused_computation.97 | convolution fusion | flops 16911433728 | bytes 30343168 | tf_op jit(solution)/vmap(transpose(jvp()))/dot_general | solution.py:20
  592.0 35.2 %fusion.36 = (f32[4096]{0:T(1024)S(1)}, bf16[4096,896]{0,1:T(8,128)(2,1)}) fusion(bf16[1,4096,896]{1,2,0:T(8,128)(2,1)} %copy.1, bf16[4096,896]{0,1:T(8,128)(2,1)} %fusion.95, bf16[1,896,2304]{2,1,0:T(8,128)(2,1)} %all-gather.32.cloned.1.call-done, bf16[1,1,4096,2304]{3,2,1,0:T(8,128)(2,1)} %fusion.25, f32[4096,2304]{1,0:T(8,128)} %fusion.97), kind=kOutput, calls=%fused_computation.58 | convolution fusion | flops 16990072832 | bytes 82788352 | tf_op jit(solution)/vmap(transpose(jvp()))/dot_general | solution.py:21
  627.9 29.1 %fusion.73 = f32[1,896,2304]{2,1,0:T(8,128)} fusion(bf16[1,1,4096,2304]{3,2,1,0:T(8,128)(2,1)} %fusion.25, f32[4096,2304]{1,0:T(8,128)} %fusion.97, bf16[1,4096,896]{1,2,0:T(8,128)(2,1)} %copy.1, f32[4096]{0:T(1024)S(1)} %bitcast.266), kind=kOutput, calls=%fused_computation.83 | convolution fusion | flops 16979066880 | bytes 72237056 | tf_op jit(solution)/vmap(transpose(jvp()))/dot_general | solution.py:21
  657.1 24.1 %convolution_bitcast_fusion = f32[1,896,2304]{2,1,0:T(8,128)} fusion(bf16[4096,2304]{1,0:T(8,128)(2,1)} %copy-done.1, bf16[1,1,4096,896]{2,3,1,0:T(8,128)(2,1)} %get-tuple-element.15, f32[4096]{0:T(1024)S(1)} %bitcast.265), kind=kOutput, calls=%fused_computation.81 | convolution fusion | flops 16922443776 | bytes 34488320 | tf_op jit(solution)/vmap(transpose(jvp()))/dot_general | solution.py:20
  681.4 24.4 %fusion.62 = f32[1,896,2304]{2,1,0:T(8,128)} fusion(bf16[4096,2304]{1,0:T(8,128)(2,1)} %fusion.7, bf16[1,4096,896]{1,2,0:T(8,128)(2,1)} %copy.1, f32[4096]{0:T(1024)S(1)} %bitcast.267), kind=kOutput, calls=%fused_computation.79 | convolution fusion | flops 16922443776 | bytes 34488320 | tf_op jit(solution)/vmap(transpose(jvp()))/dot_general | solution.py:20
  751.6 74.4 %reduce-scatter.19.cloned.1.call-done = f32[1,224,2304]{2,1,0:T(8,128)} async-done(((f32[1,896,2304]{2,1,0:T(8,128)}), f32[1,224,2304]{2,1,0:T(8,128)}) %reduce-scatter.19.cloned.1.call-update) | async-done | bytes 2064400
  827.7 75.7 %reduce-scatter.21.cloned.1.call-done = f32[1,224,2304]{2,1,0:T(8,128)} async-done(((f32[1,896,2304]{2,1,0:T(8,128)}), f32[1,224,2304]{2,1,0:T(8,128)}) %reduce-scatter.21.cloned.1.call-update) | async-done | bytes 2064400
  (77 shorter events, 146.7 us)
Async XLA Ops:
  7.2 49.6 %all-gather.30.cloned.1.call-start = ((), (), s32[]{:S(2)}) async-start(), calls=%async_computation.6 | async-start | bytes 5160960 | tf_op jit(solution)/vmap(jvp())/squeeze | solution.py:27
  10.3 92.4 %all-gather.32.cloned.1.call-start = ((), (), s32[]{:S(2)}) async-start(), calls=%async_computation.7 | async-start | bytes 5160960 | tf_op jit(solution)/vmap(jvp())/squeeze | solution.py:27
  13.4 147.7 %all-gather.34.cloned.1.call-start = ((), (), s32[]{:S(2)}) async-start(), calls=%async_computation.8 | async-start | bytes 5160960 | tf_op jit(solution)/vmap(jvp())/squeeze | solution.py:27
  16.5 177.4 %all-gather.36.cloned.1.call-start = ((), (), s32[]{:S(2)}) async-start(), calls=%async_computation.9 | async-start | bytes 5160960 | tf_op jit(solution)/vmap(jvp())/squeeze | solution.py:27
  17.2 222.5 %all-gather.40.cloned.1.call-start = ((), (), s32[]{:S(2)}) async-start(), calls=%async_computation.11 | async-start | bytes 5160960 | tf_op jit(solution)/vmap(jvp())/squeeze | solution.py:27
  17.8 267.1 %all-gather.38.cloned.1.call-start = ((), (), s32[]{:S(2)}) async-start(), calls=%async_computation.10 | async-start | bytes 5160960 | tf_op jit(solution)/vmap(jvp())/squeeze | solution.py:27
  18.5 710.5 %reduce-scatter.29.cloned.1.call-start = ((), (), s32[]{:S(2)}) async-start(), calls=%async_computation.17 | async-start | bytes 10321920
  185.8 0.6 copy-start.2
  186.4 53.3 %copy-start.4 = (f32[1,1,4096]{2,1,0:T(1,128)}, f32[1,1,4096]{2,1,0:T(1,128)S(1)}, u32[]{:S(2)}) copy-start(f32[1,1,4096]{2,1,0:T(1,128)S(1)} %rsqrt.23) | copy-start | bytes 49156
  311.4 37.1 %copy-start.10 = (bf16[1,896,2304]{2,1,0:T(8,128)(2,1)S(1)}, bf16[1,896,2304]{2,1,0:T(8,128)(2,1)}, u32[]{:S(2)}) copy-start(bf16[1,896,2304]{2,1,0:T(8,128)(2,1)} %all-gather.36.cloned.1.call-done) | copy-start | bytes 12386308
  342.1 6.4 copy-start.1
  367.6 35.0 %copy-start.3 = (f32[4096]{0:T(1024)S(1)}, f32[4096]{0:T(1024)}, u32[]{:S(2)}) copy-start(f32[4096]{0:T(1024)} %copy-done.2) | copy-start | bytes 49156
  367.6 35.0 %copy-start.5 = (f32[1,1,4096]{2,1,0:T(1,128)S(1)}, f32[1,1,4096]{2,1,0:T(1,128)}, u32[]{:S(2)}) copy-start(f32[1,1,4096]{2,1,0:T(1,128)} %copy-done.4) | copy-start | bytes 49156
  412.5 2.9 copy-start
  440.2 290.5 %reduce-scatter.27.cloned.1.call-start = ((), (), s32[]{:S(2)}) async-start(), calls=%async_computation.16 | async-start | bytes 10321920
  474.9 258.9 %reduce-scatter.23.cloned.1.call-start = ((), (), s32[]{:S(2)}) async-start(), calls=%async_computation.14 | async-start | bytes 10321920
  502.4 37.7 %copy-start.6 = (f32[1,1,4096]{2,1,0:T(1,128)S(1)}, f32[1,1,4096]{2,1,0:T(1,128)}, u32[]{:S(2)}) copy-start(f32[1,1,4096]{2,1,0:T(1,128)} %copy-done.4) | copy-start | bytes 49156
  569.0 179.5 %reduce-scatter.25.cloned.1.call-start = ((), (), s32[]{:S(2)}) async-start(), calls=%async_computation.15 | async-start | bytes 10321920
  592.0 35.2 %copy-start.9 = (f32[4096]{0:T(1024)S(1)}, f32[4096]{0:T(1024)}, u32[]{:S(2)}) copy-start(f32[4096]{0:T(1024)} %get-tuple-element.12) | copy-start | bytes 49156
  627.9 29.3 %copy-start.7 = (f32[1,1,4096]{2,1,0:T(1,128)S(1)}, f32[1,1,4096]{2,1,0:T(1,128)}, u32[]{:S(2)}) copy-start(f32[1,1,4096]{2,1,0:T(1,128)} %copy-done.4) | copy-start | bytes 49156
  657.0 169.0 %reduce-scatter.19.cloned.1.call-start = ((), (), s32[]{:S(2)}) async-start(), calls=%async_computation.12 | async-start | bytes 10321920
  681.3 24.5 %copy-start.8 = (f32[1,1,4096]{2,1,0:T(1,128)S(1)}, f32[1,1,4096]{2,1,0:T(1,128)}, u32[]{:S(2)}) copy-start(f32[1,1,4096]{2,1,0:T(1,128)} %get-tuple-element.11) | copy-start | bytes 49156
  681.3 222.1 %reduce-scatter.21.cloned.1.call-start = ((), (), s32[]{:S(2)}) async-start(), calls=%async_computation.13 | async-start | bytes 10321920
Sparse Core Ops, SparseCore 0:
  10.5 46.2 all-gather.29
  58.9 43.7 all-gather.31
  104.3 43.7 all-gather.33
  150.1 43.7 all-gather.35
  195.9 43.7 all-gather.39
  241.1 43.7 all-gather.37
  440.3 75.7 reduce-scatter.28
  518.6 75.0 reduce-scatter.26
  596.0 75.0 reduce-scatter.22
  673.4 75.0 reduce-scatter.24
  750.9 75.0 reduce-scatter.18
  828.2 75.0 reduce-scatter.20
where the time goes:
time: 924 us; the launch traced here: 914 us
  matrix products  464 us (50%)
  waiting for transfers between devices  240 us (26%)
  other arithmetic  143 us (15%)
  local copies, waits for them, and re-layouts  51.3 us (6%)
  between operations  14.8 us (2%)
    dot_general x6, matrix products, layer(): up = jnp.dot(a, w['w_up'], preferred_element_type=jnp.float32)  182 us
    unnamed x18, waiting for transfers between devices  165 us
    dot_general x6, matrix products, layer(): gate = jnp.dot(a, w['w_gate'], preferred_element_type=jnp.float32)  144 us
    dot_general x5, matrix products, matmul(): jnp.dot(a, w, preferred_element_type=jnp.float32).astype(jnp.bfloat16)  138 us
    unnamed x3, other arithmetic  100 us
    squeeze x6, waiting for transfers between devices, stack(): h = layer(h, {name: w[number] for name, w in weights.items()})  75 us
    unnamed x25, local copies, waits for them, and re-layouts  42.3 us
  transfers between devices with their start and end apart: 12, of which 8 were waited for; matrix products, arithmetic and copies ran while one was open for 54% of the time, Pallas kernels for 0%

commit v1 on v0

v1 whole, which is shorter than its diff:
```python
import functools

import jax
import jax.numpy as jnp
from jax import lax
from jax.experimental import pallas as pl
from jax.experimental.pallas import tpu as pltpu
from jax.sharding import PartitionSpec as P

F32, BF16 = jnp.float32, jnp.bfloat16
ANY = pl.BlockSpec(memory_space=pl.ANY)


def nn(a, b):
    return jnp.dot(a, b, preferred_element_type=F32)


def nt(a, b):
    return lax.dot_general(a, b, (((1,), (1,)), ((), ())), preferred_element_type=F32)


def scale_of(wide):
    return lax.rsqrt(jnp.mean(wide**2, -1, keepdims=True) + 1e-6)


def sigmoid(x):
    return 1.0 / (1.0 + jnp.exp(-x))


def fetch(pairs, sems):
    copies = [pltpu.make_async_copy(source, whole, sems.at[at]) for at, (source, whole) in enumerate(pairs)]
    for c in copies:
        c.start()
    for c in copies:
        c.wait()


def chunks(width, size):
    return [slice(at, min(at + size, width)) for at in range(0, width, size)]


def params(mb=60):
    return pltpu.CompilerParams(dimension_semantics=("arbitrary",), vmem_limit_bytes=mb * 1024 * 1024)


def cost(flops, nbytes):
    return pl.CostEstimate(flops=int(flops), bytes_accessed=int(nbytes), transcendentals=0)


def rows_spec(bm, d):
    return pl.BlockSpec((bm, d), lambda i: (i, 0))


MESH = pl.DeviceIdType.MESH


class Unit:
    def __init__(self, place, whole, own, layer, columns, parts, send, recv):
        core, left, me, right, opposite, there = place
        self.whole, self.columns, self.core, self.me = whole.at[layer], columns, core, me
        self.rows = own.shape[1]
        half = self.rows // 2
        self.number = 0

        def view(owner, part):
            rows, cols = part
            at = pl.multiple_of(owner * self.rows + core * half + rows[0], 16)
            return self.whole.at[pl.ds(at, rows[1]), cols]

        def copy(source, target, to):
            at = self.number
            self.number += 1
            return pltpu.make_async_remote_copy(source, target, send.at[at], recv.at[at], device_id=there[to], device_id_type=MESH)

        everything = ((0, half), columns)
        mine = own.at[layer, pl.ds(pl.multiple_of(core * half, 16), half), columns]
        self.first = [copy(mine, view(me, everything), to) for to in ("left", "right")]
        self.onward = [copy(view(frm, part), view(frm, part), to) for frm, part, to in ((right, parts[0], "left"), (left, parts[1], "right"))]
        self.across = [copy(view(frm, everything), view(frm, everything), "partner") for frm in (right, left)]
        self.last = [copy(view(opposite, everything), view(opposite, everything), "partner")]

    def start(self):
        for c in self.first:
            c.start()

    def pump(self):
        for c, on, over in zip(self.first, self.onward, self.across, strict=True):
            c.wait_recv()
            on.start()
            over.start()

    def finish(self):
        for c in self.onward:
            c.wait_recv()
        for c in self.last:
            c.start()

    def arrived(self):
        for c in self.across + self.last:
            c.wait_recv()

    def sent(self):
        for c in self.first + self.onward + self.across + self.last:
            c.wait_send()


COPIES = 7


def forward(x, w_gate, w_up, w_down, n, bm=256, pieces=2, cw=384):
    t, d = x.shape
    layers, _, f = w_gate.shape
    width = f // pieces
    tiles = t // bm
    halves = [w_gate.shape[1] // 2, w_down.shape[1] // 2]
    units = []

    def split(columns, rows):
        size = columns.stop - columns.start
        middle = columns.start + -(-(size // 128) // 2) * 128
        return [((0, rows), slice(columns.start, middle)), ((0, rows), slice(middle, columns.stop))]

    for p in range(pieces):
        columns = slice(p * width, (p + 1) * width)
        units += [(which, 0, columns, split(columns, halves[0])) for which in (0, 1)]
    whole_d = slice(0, d)
    by_rows = [((0, halves[1] // 2), whole_d), ((halves[1] // 2, halves[1] // 2), whole_d)]
    units.append((2, 0, whole_d, by_rows))
    for layer in range(1, layers):
        whole_f = slice(0, f)
        units += [(which, layer, whole_f, split(whole_f, halves[0])) for which in (0, 1)]
        units.append((2, layer, whole_d, by_rows))
    count = len(units)

    sizes = [(u[2].stop - u[2].start) * halves[0 if u[0] < 2 else 1] * 2 / 46e3 for u in units]
    order = [("s", 0), ("s", 1), ("f", 0), ("f", 1), ("s", 2), ("s", 3)]
    for k in range(2, count):
        order.append(("f", k))
        if k + 2 < count:
            order.append(("s", k + 2))
    clock, due = 3.0, {}
    for kind, k in order:
        clock += sizes[k] * (1.0 if kind == "s" else 0.5)
        due[kind, k] = clock + 2.0
    begin = due["f", 1] + 3.0
    pace = 52.0 / (pieces * tiles)
    steps = (pieces + 1) * tiles

    def step_of(time):
        return min(max(int((time - begin) / pace) + 1, 1), steps - 1)

    need = {2 * p + w: p * tiles for p in range(pieces) for w in (0, 1)} | {2 * pieces: pieces * tiles}
    events = []
    floor = 1
    for k in range(2, count):
        floor = max(floor, min(step_of(due["s", k]), need.get(k, steps - 1)))
        events.append((floor, "pump", k))
    late = {k: max(at, min(step_of(due["f", k]), need.get(k, steps - 1))) for at, _, k in events}

    def kernel(x_ref, gs, us, ds, at_ref, g_ref, u_ref, h_ref, wg, wu, wd, hidden, vg, vu, vd, og, ou, od, local, send, recv):
        i = pl.program_id(0)
        rep, me = lax.axis_index("rep"), lax.axis_index("dp")
        core = lax.rem(rep, 2)
        other = rep + 1 - 2 * core
        left, right, opposite = lax.rem(me + n - 1, n), lax.rem(me + 1, n), lax.rem(me + 2, n)
        there = {"left": (rep, left), "right": (rep, right), "partner": (other, me)}
        place = (core, left, me, right, opposite, there)
        wholes, owns = (wg, wu, wd), (og, ou, od)
        flows = [
            Unit(place, wholes[which], owns[which], layer, columns, parts, send.at[at], recv.at[at])
            for at, (which, layer, columns, parts) in enumerate(units)
        ]
        keep = []
        for which in range(3):
            rows = owns[which].shape[1]
            for layer in range(layers):
                target = wholes[which].at[layer, pl.ds(pl.multiple_of(me * rows, 16), rows)]
                keep.append(pltpu.make_async_copy(owns[which].at[layer], target, local.at[3 + len(keep)]))

        @pl.when(i == 0)
        def _():
            fetch(((gs, og), (us, ou), (ds, od)), local)
            barrier = pltpu.get_barrier_semaphore()
            for to in there.values():
                pl.semaphore_signal(barrier, inc=1, device_id=to, device_id_type=MESH)
            pl.semaphore_wait(barrier, len(there))
            flows[0].start()
            flows[1].start()
            for c in keep:
                c.start()
            flows[0].pump()
            flows[1].pump()
            flows[2].start()
            flows[3].start()
            for c in keep:
                c.wait()
            for flow in flows[:2]:
                flow.finish()
            for flow in flows[:2]:
                flow.arrived()

        for step in range(1, steps):
            pumps = [k for at, _, k in events if at == step]
            ends = [k for k in late if late[k] == step]
            if pumps or ends:

                @pl.when(i == step)
                def _(pumps=pumps, ends=ends):
                    for k in pumps:
                        flows[k].pump()
                        if k + 2 < count:
                            flows[k + 2].start()
                    for k in ends:
                        flows[k].finish()

        for p in range(pieces):

            @pl.when(i == p * tiles)
            def _(p=p):
                if p:
                    flows[2 * p].arrived()
                    flows[2 * p + 1].arrived()
                columns = pl.ds(p * width, width)
                fetch(((wg.at[0, :, columns], vg.at[:, columns]), (wu.at[0, :, columns], vu.at[:, columns])), local)

        @pl.when(i == pieces * tiles)
        def _():
            flows[2 * pieces].arrived()
            fetch(((wd.at[0], vd),), local)

        for p in range(pieces):

            @pl.when(i // tiles == p)
            def _(p=p):
                wide = x_ref[...].astype(F32)
                a = (wide * scale_of(wide)).astype(BF16)
                if p == 0:
                    at_ref[...] = a.T
                rows = pl.ds(pl.multiple_of((i - p * tiles) * bm, bm), bm)
                for c in chunks(width, cw):
                    from_all = slice(p * width + c.start, p * width + c.stop)
                    g = nn(a, vg[:, from_all])
                    u = nn(a, vu[:, from_all])
                    g_ref[:, c] = g
                    u_ref[:, c] = u
                    hidden[rows, from_all] = (g * sigmoid(g) * u).astype(BF16)

        @pl.when(i // tiles == pieces)
        def _():
            rows = pl.ds(pl.multiple_of((i - pieces * tiles) * bm, bm), bm)
            h_ref[...] = x_ref[...] + nn(hidden[rows, :], vd[...]).astype(BF16)

        @pl.when(i == steps - 1)
        def _():
            for flow in flows[2 * pieces + 1 :]:
                flow.arrived()
            for flow in flows:
                flow.sent()

    def tile(i):
        return lax.rem(i, tiles)

    last = pieces * tiles - 1
    once = pl.BlockSpec((bm, width), lambda i: (tile(jnp.minimum(i, last)), jnp.minimum(i, last) // tiles))
    return pl.pallas_call(
        kernel,
        grid=(steps,),
        in_specs=[pl.BlockSpec((bm, d), lambda i: (tile(i), 0)), ANY, ANY, ANY],
        out_specs=[
            pl.BlockSpec((d, bm), lambda i: (0, jnp.minimum(i, tiles - 1))),
            once,
            once,
            pl.BlockSpec((bm, d), lambda i: (jnp.maximum(i - pieces * tiles, 0), 0)),
            ANY,
            ANY,
            ANY,
        ],
        out_shape=[
            jax.ShapeDtypeStruct((d, t), BF16),
            jax.ShapeDtypeStruct((t, f), F32),
            jax.ShapeDtypeStruct((t, f), F32),
            jax.ShapeDtypeStruct((t, d), BF16),
            jax.ShapeDtypeStruct((layers, d, f), BF16),
            jax.ShapeDtypeStruct((layers, d, f), BF16),
            jax.ShapeDtypeStruct((layers, f, d), BF16),
        ],
        scratch_shapes=[
            pltpu.VMEM((t, f), BF16),
            pltpu.VMEM((d, f), BF16),
            pltpu.VMEM((d, f), BF16),
            pltpu.VMEM((f, d), BF16),
            pltpu.VMEM(w_gate.shape, BF16),
            pltpu.VMEM(w_up.shape, BF16),
            pltpu.VMEM(w_down.shape, BF16),
            pltpu.SemaphoreType.DMA((3 + 3 * layers,)),
            pltpu.SemaphoreType.DMA((count, COPIES)),
            pltpu.SemaphoreType.DMA((count, COPIES)),
        ],
        compiler_params=pltpu.CompilerParams(
            dimension_semantics=("arbitrary",), vmem_limit_bytes=62 * 1024 * 1024, collective_id=0, has_side_effects=True
        ),
        cost_estimate=cost(6 * t * d * f, t * f * 8 + t * d * 8),
        name="forward",
    )(x, w_gate, w_up, w_down)


class Scatter:
    @staticmethod
    def halves(rows, columns):
        if columns // 2 % 128 == 0:
            return [(slice(0, rows), slice(0, columns // 2)), (slice(0, rows), slice(columns // 2, columns))]
        return [(slice(0, rows // 2), slice(0, columns)), (slice(rows // 2, rows), slice(0, columns))]

    @staticmethod
    def scratch(term, n):
        rows, columns = term.shape[0] // n, term.shape[1]
        r, c = Scatter.halves(rows, columns)[0]
        half = (r.stop - r.start, c.stop - c.start)
        return [
            pltpu.VMEM((6, *half), BF16),
            pltpu.VMEM((4, *half), BF16),
            pltpu.VMEM((rows, columns), BF16),
            pltpu.SemaphoreType.DMA((3,)),
            pltpu.SemaphoreType.DMA((6,)),
            pltpu.SemaphoreType.DMA((6,)),
        ]

    def __init__(self, n, term, out, came, own, mine, local, send, recv):
        rep, me = lax.axis_index("rep"), lax.axis_index("dp")
        left, right, opposite = lax.rem(me + n - 1, n), lax.rem(me + 1, n), lax.rem(me + 2, n)
        rows = term.shape[0] // n
        self.out, self.came, self.own, self.mine = out, came, own, mine
        self.parts = first, second = self.halves(rows, term.shape[1])

        def of(owner, part):
            r, c = part
            at = pl.multiple_of(owner * rows + r.start, 16)
            return term.at[pl.ds(at, r.stop - r.start), c]

        def copy(source, at, to):
            return pltpu.make_async_remote_copy(
                source, came.at[at], send.at[at], recv.at[at], device_id=(rep, to), device_id_type=MESH
            )

        self.far = [copy(of(opposite, first), 0, right), copy(of(opposite, second), 1, left)]
        self.near = [copy(of(right, second), 2, right), copy(of(left, first), 3, left)]
        self.sums = [copy(own.at[2], 4, right), copy(own.at[3], 5, left)]
        self.loads = [
            pltpu.make_async_copy(of(right, first), own.at[0], local.at[0]),
            pltpu.make_async_copy(of(left, second), own.at[1], local.at[1]),
            pltpu.make_async_copy(term.at[pl.ds(pl.multiple_of(me * rows, 16), rows)], mine, local.at[2]),
        ]

    def begin(self):
        for c in self.far:
            c.start()
        for c in self.loads:
            c.start()

    def neighbours(self):
        for c in self.near:
            c.start()

    def add(self):
        for c in self.loads:
            c.wait()
        for c in self.far:
            c.wait_recv()
        for at in (0, 1):
            self.own[2 + at] = (self.own[at].astype(F32) + self.came[at].astype(F32)).astype(BF16)

    def pass_on(self):
        for c in self.sums:
            c.start()

    def end(self):
        for c in self.near + self.sums:
            c.wait_recv()
        for part, from_left, from_right in zip(self.parts, (4, 2), (3, 5), strict=True):
            total = self.mine[part].astype(F32) + self.came[from_left].astype(F32) + self.came[from_right].astype(F32)
            self.out[part] = total.astype(BF16)
        for c in self.far + self.near + self.sums:
            c.wait_send()


SCATTER = 6


def greet(n):
    rep, me = lax.axis_index("rep"), lax.axis_index("dp")
    barrier = pltpu.get_barrier_semaphore()
    for to in (lax.rem(me + n - 1, n), lax.rem(me + 1, n)):
        pl.semaphore_signal(barrier, inc=1, device_id=(rep, to), device_id_type=MESH)
    pl.semaphore_wait(barrier, 2)


def scattering(kernel, n, terms, plan, identity, grid, in_specs, out_specs, out_shape, scratch_shapes, name, flops, nbytes):
    steps = grid[0]
    ins, outs = len(in_specs), len(out_specs)
    given = [Scatter.scratch(term, n) for term in terms]

    def whole(*refs):
        i = pl.program_id(0)
        own_in, refs = refs[:ins], refs[ins:]
        term_refs, refs = refs[: len(terms)], refs[len(terms) :]
        own_out, refs = refs[:outs], refs[outs:]
        shard_refs, refs = refs[: len(terms)], refs[len(terms) :]
        own_scratch, refs = refs[: len(scratch_shapes)], refs[len(scratch_shapes) :]
        flows = [
            Scatter(n, term, shard, *refs[at * SCATTER : (at + 1) * SCATTER])
            for at, (term, shard) in enumerate(zip(term_refs, shard_refs, strict=True))
        ]

        @pl.when(i == 0)
        def _():
            greet(n)
            for step, action, which in plan:
                if step == 0:
                    getattr(flows[which], action)()

        for step in sorted({p[0] for p in plan if p[0]}):

            @pl.when(i == step)
            def _(step=step):
                for at, action, which in plan:
                    if at == step:
                        getattr(flows[which], action)()

        kernel(*own_in, *own_out, *own_scratch)

        @pl.when(i == steps - 1)
        def _():
            for flow in flows:
                flow.end()

    shards = [(term.shape[0] // n, term.shape[1]) for term in terms]
    return lambda *operands: pl.pallas_call(
        whole,
        grid=grid,
        in_specs=list(in_specs) + [ANY] * len(terms),
        out_specs=list(out_specs) + [pl.BlockSpec(shard, lambda i: (0, 0)) for shard in shards],
        out_shape=list(out_shape) + [jax.ShapeDtypeStruct(shard, BF16) for shard in shards],
        scratch_shapes=list(scratch_shapes) + [x for one in given for x in one],
        compiler_params=pltpu.CompilerParams(
            dimension_semantics=("arbitrary",),
            vmem_limit_bytes=62 * 1024 * 1024,
            collective_id=identity,
            has_side_effects=True,
        ),
        cost_estimate=cost(flops, nbytes),
        name=name,
    )(*operands, *terms)


ONE = ((0, "begin", 0), (0, "neighbours", 0), (5, "add", 0), (6, "pass_on", 0))
TWO = (
    (0, "begin", 0), (0, "neighbours", 0), (0, "begin", 1),
    (5, "add", 0), (6, "pass_on", 0), (6, "neighbours", 1),
    (11, "add", 1), (12, "pass_on", 1),
)


def to_gates(g, u, dh):
    s = sigmoid(g)
    silu = g * s
    return (dh * u * (s + silu * (1.0 - s))).astype(BF16), (dh * silu).astype(BF16), (silu * u).astype(BF16)


def finish_down(acc, o_ref, cw=256):
    for c in chunks(acc.shape[1], cw):
        o_ref[c, :] = acc[:, c].T.astype(BF16)


def top_layer(h, dy, gate, up, down, layer, bm=512, cw=768):
    t, d = h.shape
    f = gate.shape[2]

    def kernel(h_ref, dy_ref, gw, uw, dw, at_ref, dg_ref, du_ref, o_ref, wg, wu, wd, acc, sems):
        i = pl.program_id(0)

        @pl.when(i == 0)
        def _():
            fetch(((gw.at[layer], wg), (uw.at[layer], wu), (dw.at[layer], wd)), sems)
            acc[...] = jnp.zeros_like(acc)

        wide = h_ref[...].astype(F32)
        a = (wide * scale_of(wide)).astype(BF16)
        at_ref[...] = a.T
        by = dy_ref[...]
        by_t = by.T
        for c in chunks(f, cw):
            g = nn(a, wg[:, c])
            u = nn(a, wu[:, c])
            dh = nt(by, wd[c, :]).astype(BF16).astype(F32)
            dg, du, hidden = to_gates(g, u, dh)
            dg_ref[:, c] = dg
            du_ref[:, c] = du
            acc[:, c] += nn(by_t, hidden)

        @pl.when(i == pl.num_programs(0) - 1)
        def _():
            finish_down(acc, o_ref)

    return pl.pallas_call(
        kernel,
        grid=(t // bm,),
        in_specs=[rows_spec(bm, d), rows_spec(bm, d)] + [ANY] * 3,
        out_specs=[
            pl.BlockSpec((d, bm), lambda i: (0, i)),
            rows_spec(bm, f),
            rows_spec(bm, f),
            pl.BlockSpec((f, d), lambda i: (0, 0)),
        ],
        out_shape=[
            jax.ShapeDtypeStruct((d, t), BF16),
            jax.ShapeDtypeStruct((t, f), BF16),
            jax.ShapeDtypeStruct((t, f), BF16),
            jax.ShapeDtypeStruct((f, d), BF16),
        ],
        scratch_shapes=[
            pltpu.VMEM((d, f), BF16),
            pltpu.VMEM((d, f), BF16),
            pltpu.VMEM((f, d), BF16),
            pltpu.VMEM((d, f), F32),
            pltpu.SemaphoreType.DMA((3,)),
        ],
        compiler_params=params(),
        cost_estimate=cost(8 * t * d * f, t * f * 4 + t * d * 6),
        name="top_layer",
    )(h, dy, gate, up, down)


def low_layer(n, terms, identity, g, u, dy, down, layer, bm=256, cw=768):
    t, f = g.shape
    d = dy.shape[1]

    def kernel(g_ref, u_ref, dy_ref, dw, dg_ref, du_ref, o_ref, wd, acc, sems):
        i = pl.program_id(0)

        @pl.when(i == 0)
        def _():
            fetch(((dw.at[layer], wd),), sems)
            acc[...] = jnp.zeros_like(acc)

        by = dy_ref[...]
        by_t = by.T
        for c in chunks(f, cw):
            dh = nt(by, wd[c, :]).astype(BF16).astype(F32)
            dg, du, hidden = to_gates(g_ref[:, c], u_ref[:, c], dh)
            dg_ref[:, c] = dg
            du_ref[:, c] = du
            acc[:, c] += nn(by_t, hidden)

        @pl.when(i == pl.num_programs(0) - 1)
        def _():
            finish_down(acc, o_ref)

    return scattering(
        kernel, n, terms, ONE, identity,
        grid=(t // bm,),
        in_specs=[rows_spec(bm, f), rows_spec(bm, f), rows_spec(bm, d), ANY],
        out_specs=[rows_spec(bm, f), rows_spec(bm, f), pl.BlockSpec((f, d), lambda i: (0, 0))],
        out_shape=[
            jax.ShapeDtypeStruct((t, f), BF16),
            jax.ShapeDtypeStruct((t, f), BF16),
            jax.ShapeDtypeStruct((f, d), BF16),
        ],
        scratch_shapes=[pltpu.VMEM((f, d), BF16), pltpu.VMEM((d, f), F32), pltpu.SemaphoreType.DMA((1,))],
        name="low_layer", flops=4 * t * d * f, nbytes=t * f * 12 + t * d * 2,
    )(g, u, dy, down)


def weight_grads(n, terms, identity, at, dg, du, bt=512):
    d, t = at.shape
    f = dg.shape[1]
    tiles = t // bt

    def kernel(a_ref, g_ref, u_ref, og_ref, ou_ref, acc):
        i = pl.program_id(0)
        for first, x_ref, o_ref in ((0, g_ref, og_ref), (tiles, u_ref, ou_ref)):
            last = first + tiles - 1

            @pl.when(i == first)
            def _(x_ref=x_ref):
                acc[...] = nn(a_ref[...], x_ref[...])

            @pl.when((i > first) & (i < last))
            def _(x_ref=x_ref):
                acc[...] += nn(a_ref[...], x_ref[...])

            @pl.when(i == last)
            def _(x_ref=x_ref, o_ref=o_ref):
                o_ref[...] = (acc[...] + nn(a_ref[...], x_ref[...])).astype(BF16)

    return scattering(
        kernel, n, terms, ONE, identity,
        grid=(2 * tiles,),
        in_specs=[
            pl.BlockSpec((d, bt), lambda i: (0, lax.rem(i, tiles))),
            pl.BlockSpec((bt, f), lambda i: (jnp.minimum(i, tiles - 1), 0)),
            pl.BlockSpec((bt, f), lambda i: (jnp.maximum(i - tiles, 0), 0)),
        ],
        out_specs=[pl.BlockSpec((d, f), lambda i: (0, 0))] * 2,
        out_shape=[jax.ShapeDtypeStruct((d, f), BF16)] * 2,
        scratch_shapes=[pltpu.VMEM((d, f), F32)],
        name="weight_grads", flops=4 * t * d * f, nbytes=t * f * 4 + t * d * 4 + d * f * 4,
    )(at, dg, du)


def input_grad(n, terms, plan, identity, dg, du, h, dy, gate, up, layer, bm=256):
    t, d = h.shape
    f = dg.shape[1]

    def kernel(dg_ref, du_ref, h_ref, dy_ref, gw, uw, o_ref, wg, wu, sems):
        @pl.when(pl.program_id(0) == 0)
        def _():
            fetch(((gw.at[layer], wg), (uw.at[layer], wu)), sems)

        da = (nt(dg_ref[...], wg[...]) + nt(du_ref[...], wu[...])).astype(BF16).astype(F32)
        wide = h_ref[...].astype(F32)
        scale = scale_of(wide)
        along = jnp.mean(da * wide, -1, keepdims=True)
        dh = da * scale - wide * (scale * scale * scale * along)
        o_ref[...] = dy_ref[...] + dh.astype(BF16)

    return scattering(
        kernel, n, terms, plan, identity,
        grid=(t // bm,),
        in_specs=[rows_spec(bm, f), rows_spec(bm, f), rows_spec(bm, d), rows_spec(bm, d), ANY, ANY],
        out_specs=[rows_spec(bm, d)],
        out_shape=[jax.ShapeDtypeStruct((t, d), BF16)],
        scratch_shapes=[pltpu.VMEM((d, f), BF16), pltpu.VMEM((d, f), BF16), pltpu.SemaphoreType.DMA((2,))],
        name="input_grad", flops=4 * t * d * f, nbytes=t * f * 4 + t * d * 6,
    )(dg, du, h, dy, gate, up)


def solution(mesh):
    n = mesh.shape["dp"]

    def body(x, dy, w_gate, w_up, w_down):
        shape = x.shape
        x, dy = (v.reshape(v.shape[-2:]) for v in (x, dy))
        at0, g0, u0, h1, gate, up, down = forward(x, w_gate, w_up, w_down, n)
        at1, dg1, du1, dwd1 = top_layer(h1, dy, gate, up, down, 1)
        dwg1, dwu1, down1 = weight_grads(n, [dwd1], 1, at1, dg1, du1)
        dh1, gate1 = input_grad(n, [dwg1], ONE, 2, dg1, du1, h1, dy, gate, up, 1)
        dg0, du0, dwd0, up1 = low_layer(n, [dwu1], 3, g0, u0, dh1, down, 0)
        dwg0, dwu0, down0 = weight_grads(n, [dwd0], 4, at0, dg0, du0)
        dx, gate0, up0 = input_grad(n, [dwg0, dwu0], TWO, 5, dg0, du0, x, dh1, gate, up, 0)
        return dx.reshape(shape), jnp.stack([gate0, gate1]), jnp.stack([up0, up1]), jnp.stack([down0, down1])

    seq, row = P(("rep", "dp")), P(None, "dp")
    out = P("rep", "dp")
    return jax.shard_map(
        body, mesh=mesh, in_specs=(seq, seq, row, row, row), out_specs=(seq, out, out, out), check_vma=False
    )
```

time: 924 us -> 536 us (0.58)
  Pallas kernels: 0 us -> 519 us
  matrix products: 464 us -> 0 us
  waiting for transfers between devices: 240 us -> 0 us
  other arithmetic: 143 us -> 7.54 us
  local copies, waits for them, and re-layouts: 51.3 us -> 3.06 us
  between operations: 14.8 us -> 1.2 us
    pallas_call x0 -> x7, Pallas kernels: none -> 519 us  [the longest x5 285 us: scattering(): pl.pallas_call(whole, grid=grid, in_specs=list(in_specs) + [ANY] * len(te...]
    dot_general x17 -> x0, matrix products: 464 us -> none  [the longest x6 182 us: layer(): up = jnp.dot(a, w['w_up'], preferred_element_type=jnp.float32)]
    unnamed x18 -> x0, waiting for transfers between devices: 165 us -> none
    unnamed x3 -> x0, other arithmetic: 100 us -> none
    squeeze x6 -> x0, waiting for transfers between devices: 75 us -> none  [stack(): h = layer(h, {name: w[number] for name, w in weights.items()})]
    unnamed x25 -> x5, local copies, waits for them, and re-layouts: 42.3 us -> 3.06 us
    reshape x4 -> x0, other arithmetic: 16.7 us -> none  [the longest x1 12.4 us: step(): by_x.reshape(shape)]
    broadcast_in_dim x6 -> x0, other arithmetic: 10.1 us -> none  [stack(): h = layer(h, {name: w[number] for name, w in weights.items()})]
  transfers between devices with their start and end apart: 12 -> 0, of which waited for: 8 -> 0; matrix products, arithmetic and copies ran while one was open for 54% -> 0% of each run, Pallas kernels for 0% -> 0%
where the time goes in v1:
time: 536 us; the launch traced here: 531 us
  Pallas kernels  519 us (97%)
  other arithmetic  7.54 us (1%)
    pallas_call x5, Pallas kernels, scattering(): pl.pallas_call(whole, grid=grid, in_specs=list(in_specs) + [ANY] * len(te...  285 us
    pallas_call x1, Pallas kernels, forward(): pl.pallas_call(kernel, grid=(steps,), in_specs=[pl.BlockSpec((bm, d), lam...  140 us
    pallas_call x1, Pallas kernels, top_layer(): pl.pallas_call(kernel, grid=(t // bm,), in_specs=[rows_spec(bm, d), rows_...  94.9 us

profile of v1, /device:TPU:112, one launch (start us, length us, event | category | flops | bytes accessed | tf_op | source)
XLA Modules:
  0.0 531.1 jit_solution(27915930351506345)
XLA Ops:
  0.6 139.7 %forward.1 = (bf16[896,4096]{1,0:T(8,128)(2,1)}, f32[4096,2304]{1,0:T(8,128)}, f32[4096,2304]{1,0:T(8,128)}, bf16[4096,896]{1,0:T(8,128)(2,1)}, bf16[2,896,2304]...) custom-call(bf16[4096,896]{1,0:T(8,128)(2,1)} %bitcast.18, bf16[2,224,2304]{2,1,0:T(8,128)(2,1)} %gs.1, ...), custom_call_target="tpu_custom_call" | custom-call | flops 50734301184 | bytes 104857600 | tf_op jit(solution)/shard_map/forward/pallas_call | solution.py:265
  140.4 94.9 %top_layer.1 = (bf16[896,4096]{1,0:T(8,128)(2,1)}, bf16[4096,2304]{1,0:T(8,128)(2,1)}, bf16[4096,2304]{1,0:T(8,128)(2,1)}, bf16[2304,896]{1,0:T(8,128)(2,1)}) custom-call(bf16[4096,896]{1,0:T(8,128)(2,1)} %get-tuple-element.32.h_ref.refs_2_, bf16[4096,896]{1,0:T(8,128)(2,1)} %bitcast.16, bf16[2,896,2304]{2,1,0:T(8,128)(2,1)} %get-tuple-element.33.gw.refs_4_, ...), custom_call_target="tpu_custom_call" | custom-call | flops 67645734912 | bytes 59768832 | tf_op jit(solution)/shard_map/top_layer/pallas_call | solution.py:504
  235.2 49.8 %weight_grads.2 = (bf16[896,2304]{1,0:T(8,128)(2,1)}, bf16[896,2304]{1,0:T(8,128)(2,1)}, bf16[576,896]{1,0:T(8,128)(2,1)}) custom-call(bf16[896,4096]{1,0:T(8,128)(2,1)} %get-tuple-element.38.refs_0_, bf16[4096,2304]{1,0:T(8,128)(2,1)} %get-tuple-element.36.refs_1_.refs_0_, bf16[4096,2304]{1,0:T(8,128)(2,1)} %get-tuple-element.37.refs_2_.refs_1_, ...), custom_call_target="tpu_custom_call" | custom-call | flops 33822867456 | bytes 60686336 | tf_op jit(solution)/shard_map/weight_grads/pallas_call | solution.py:437
  285.0 54.6 %input_grad.2 = (bf16[4096,896]{1,0:T(8,128)(2,1)}, bf16[224,2304]{1,0:T(8,128)(2,1)}) custom-call(bf16[4096,2304]{1,0:T(8,128)(2,1)} %get-tuple-element.36.refs_1_.refs_0_, bf16[4096,2304]{1,0:T(8,128)(2,1)} %get-tuple-element.37.refs_2_.refs_1_, bf16[4096,896]{1,0:T(8,128)(2,1)} %get-tuple-element.32.h_ref.refs_2_, bf16[4096,896]{1,0:T(8,128)(2,1)} %bitcast.17, ...), custom_call_target="tpu_custom_call" | custom-call | flops 33822867456 | bytes 59768832 | tf_op jit(solution)/shard_map/input_grad/pallas_call | solution.py:437
  339.6 60.3 %low_layer.1 = (bf16[4096,2304]{1,0:T(8,128)(2,1)}, bf16[4096,2304]{1,0:T(8,128)(2,1)}, bf16[2304,896]{1,0:T(8,128)(2,1)}, bf16[224,2304]{1,0:T(8,128)(2,1)}) custom-call(f32[4096,2304]{1,0:T(8,128)} %get-tuple-element.30.refs_0_, f32[4096,2304]{1,0:T(8,128)} %get-tuple-element.31.refs_1_, bf16[4096,896]{1,0:T(8,128)(2,1)} %get-tuple-element.41.refs_2_.refs_3_, ...), custom_call_target="tpu_custom_call" | custom-call | flops 33822867456 | bytes 120586240 | tf_op jit(solution)/shard_map/low_layer/pallas_call | solution.py:437
  399.9 49.9 %weight_grads.3 = (bf16[896,2304]{1,0:T(8,128)(2,1)}, bf16[896,2304]{1,0:T(8,128)(2,1)}, bf16[576,896]{1,0:T(8,128)(2,1)}) custom-call(bf16[896,4096]{1,0:T(8,128)(2,1)} %get-tuple-element.45.refs_0_, bf16[4096,2304]{1,0:T(8,128)(2,1)} %get-tuple-element.43.refs_1_.refs_0_, bf16[4096,2304]{1,0:T(8,128)(2,1)} %get-tuple-element.44.refs_2_.refs_1_, ...), custom_call_target="tpu_custom_call" | custom-call | flops 33822867456 | bytes 60686336 | tf_op jit(solution)/shard_map/weight_grads/pallas_call | solution.py:437
  449.8 0.0 copy-start.1
  449.8 70.2 %input_grad.3 = (bf16[4096,896]{1,0:T(8,128)(2,1)}, bf16[224,2304]{1,0:T(8,128)(2,1)}, bf16[224,2304]{1,0:T(8,128)(2,1)}) custom-call(bf16[4096,2304]{1,0:T(8,128)(2,1)} %get-tuple-element.43.refs_1_.refs_0_, bf16[4096,2304]{1,0:T(8,128)(2,1)} %get-tuple-element.44.refs_2_.refs_1_, bf16[4096,896]{1,0:T(8,128)(2,1)} %bitcast.19, ...), custom_call_target="tpu_custom_call" | custom-call | flops 33822867456 | bytes 59768832 | tf_op jit(solution)/shard_map/input_grad/pallas_call | solution.py:437
  520.0 0.0 copy-start
  520.0 4.8 pad_maximum_fusion
  524.8 0.0 copy-done.1
  524.8 2.8 pad_maximum_fusion.2
  527.6 0.0 copy-done
  527.6 3.0 copy.10
Async XLA Ops:
  449.8 75.1 %copy-start.1 = (bf16[576,896]{1,0:T(8,128)(2,1)S(1)}, bf16[576,896]{1,0:T(8,128)(2,1)}, u32[]{:S(2)}) copy-start(bf16[576,896]{1,0:T(8,128)(2,1)} %get-tuple-element.55) | copy-start | bytes 3096580
  520.0 7.6 %copy-start = (bf16[4096,896]{1,0:T(8,128)(2,1)S(1)}, bf16[4096,896]{1,0:T(8,128)(2,1)}, u32[]{:S(2)}) copy-start(bf16[4096,896]{1,0:T(8,128)(2,1)} %get-tuple-element.49) | copy-start | bytes 22020100

commit v2 on v1

--- a/solution.py
+++ b/solution.py
@@ -107,7 +107,7 @@
 COPIES = 7
 
 
-def forward(x, w_gate, w_up, w_down, n, bm=256, pieces=2, cw=384):
+def forward(x, w_gate, w_up, w_down, n, bm=512, pieces=2, cw=1152):
     t, d = x.shape
     layers, _, f = w_gate.shape
     width = f // pieces
@@ -132,7 +132,7 @@
         units.append((2, layer, whole_d, by_rows))
     count = len(units)
 
-    sizes = [(u[2].stop - u[2].start) * halves[0 if u[0] < 2 else 1] * 2 / 46e3 for u in units]
+    sizes = [(u[2].stop - u[2].start) * halves[0 if u[0] < 2 else 1] * 2 / 60e3 for u in units]
     order = [("s", 0), ("s", 1), ("f", 0), ("f", 1), ("s", 2), ("s", 3)]
     for k in range(2, count):
         order.append(("f", k))
@@ -312,24 +312,21 @@
         return [(slice(0, rows // 2), slice(0, columns)), (slice(rows // 2, rows), slice(0, columns))]
 
     @staticmethod
-    def scratch(term, n):
-        rows, columns = term.shape[0] // n, term.shape[1]
+    def scratch(shape, n, here=False):
+        rows, columns = shape[0] // n, shape[1]
         r, c = Scatter.halves(rows, columns)[0]
         half = (r.stop - r.start, c.stop - c.start)
-        return [
-            pltpu.VMEM((6, *half), BF16),
-            pltpu.VMEM((4, *half), BF16),
-            pltpu.VMEM((rows, columns), BF16),
-            pltpu.SemaphoreType.DMA((3,)),
-            pltpu.SemaphoreType.DMA((6,)),
-            pltpu.SemaphoreType.DMA((6,)),
-        ]
-
-    def __init__(self, n, term, out, came, own, mine, local, send, recv):
+        landing = [pltpu.VMEM((6, *half), BF16), pltpu.VMEM((2, *half), BF16)]
+        if not here:
+            landing += [pltpu.VMEM((2, *half), BF16), pltpu.VMEM((rows, columns), BF16), pltpu.SemaphoreType.DMA((3,))]
+        return landing + [pltpu.SemaphoreType.DMA((6,)), pltpu.SemaphoreType.DMA((6,))]
+
+    def __init__(self, n, term, out, came, totals, *rest):
+        *loaded, send, recv = rest
         rep, me = lax.axis_index("rep"), lax.axis_index("dp")
         left, right, opposite = lax.rem(me + n - 1, n), lax.rem(me + 1, n), lax.rem(me + 2, n)
         rows = term.shape[0] // n
-        self.out, self.came, self.own, self.mine = out, came, own, mine
+        self.out, self.came, self.totals = out, came, totals
         self.parts = first, second = self.halves(rows, term.shape[1])
 
         def of(owner, part):
@@ -344,12 +341,20 @@
 
         self.far = [copy(of(opposite, first), 0, right), copy(of(opposite, second), 1, left)]
         self.near = [copy(of(right, second), 2, right), copy(of(left, first), 3, left)]
-        self.sums = [copy(own.at[2], 4, right), copy(own.at[3], 5, left)]
-        self.loads = [
-            pltpu.make_async_copy(of(right, first), own.at[0], local.at[0]),
-            pltpu.make_async_copy(of(left, second), own.at[1], local.at[1]),
-            pltpu.make_async_copy(term.at[pl.ds(pl.multiple_of(me * rows, 16), rows)], mine, local.at[2]),
-        ]
+        self.sums = [copy(totals.at[0], 4, right), copy(totals.at[1], 5, left)]
+        self.loads = []
+        if loaded:
+            own, mine, local = loaded
+            self.mine = [mine.at[part] for part in self.parts]
+            self.theirs = [own.at[0], own.at[1]]
+            self.loads = [
+                pltpu.make_async_copy(of(right, first), own.at[0], local.at[0]),
+                pltpu.make_async_copy(of(left, second), own.at[1], local.at[1]),
+                pltpu.make_async_copy(term.at[pl.ds(pl.multiple_of(me * rows, 16), rows)], mine, local.at[2]),
+            ]
+        else:
+            self.mine = [of(me, part) for part in self.parts]
+            self.theirs = [of(right, first), of(left, second)]
 
     def begin(self):
         for c in self.far:
@@ -367,7 +372,7 @@
         for c in self.far:
             c.wait_recv()
         for at in (0, 1):
-            self.own[2 + at] = (self.own[at].astype(F32) + self.came[at].astype(F32)).astype(BF16)
+            self.totals[at] = (self.theirs[at][...].astype(F32) + self.came[at].astype(F32)).astype(BF16)
 
     def pass_on(self):
         for c in self.sums:
@@ -376,14 +381,14 @@
     def end(self):
         for c in self.near + self.sums:
             c.wait_recv()
-        for part, from_left, from_right in zip(self.parts, (4, 2), (3, 5), strict=True):
-            total = self.mine[part].astype(F32) + self.came[from_left].astype(F32) + self.came[from_right].astype(F32)
+        for part, mine, from_left, from_right in zip(self.parts, self.mine, (4, 2), (3, 5), strict=True):
+            total = mine[...].astype(F32) + self.came[from_left].astype(F32) + self.came[from_right].astype(F32)
             self.out[part] = total.astype(BF16)
         for c in self.far + self.near + self.sums:
             c.wait_send()
 
 
-SCATTER = 6
+SCATTER = 7
 
 
 def greet(n):
@@ -397,7 +402,7 @@
 def scattering(kernel, n, terms, plan, identity, grid, in_specs, out_specs, out_shape, scratch_shapes, name, flops, nbytes):
     steps = grid[0]
     ins, outs = len(in_specs), len(out_specs)
-    given = [Scatter.scratch(term, n) for term in terms]
+    given = [Scatter.scratch(term.shape, n) for term in terms]
 
     def whole(*refs):
         i = pl.program_id(0)
@@ -453,12 +458,6 @@
 
 
 ONE = ((0, "begin", 0), (0, "neighbours", 0), (5, "add", 0), (6, "pass_on", 0))
-TWO = (
-    (0, "begin", 0), (0, "neighbours", 0), (0, "begin", 1),
-    (5, "add", 0), (6, "pass_on", 0), (6, "neighbours", 1),
-    (11, "add", 1), (12, "pass_on", 1),
-)
-
 
 def to_gates(g, u, dh):
     s = sigmoid(g)
@@ -570,68 +569,138 @@
     )(g, u, dy, down)
 
 
-def weight_grads(n, terms, identity, at, dg, du, bt=512):
+def back(n, identity, term, at, dg, du, h, dy, gate, up, layer, last, bt=512, inner=256):
     d, t = at.shape
     f = dg.shape[1]
     tiles = t // bt
-
-    def kernel(a_ref, g_ref, u_ref, og_ref, ou_ref, acc):
+    steps = 3 * tiles
+    middle, low = tiles, 2 * tiles
+    plan = [
+        (0, "begin", 0), (0, "neighbours", 0), (5, "add", 0), (6, "pass_on", 0), (middle + 5, "end", 0),
+        (middle, "begin", 1), (middle, "neighbours", 1), (low + 1, "add", 1), (low + 2, "pass_on", 1), (low + 5, "end", 1),
+    ]
+    if last:
+        plan += [(low, "begin", 2), (low + 2, "neighbours", 2), (low + 4, "add", 2), (low + 5, "pass_on", 2)]
+
+    def kernel(at_ref, dg_ref, du_ref, h_ref, dy_ref, gw, uw, down_term, o_ref, down_out, gate_out, up_out, *scratch):
+        acc, gate_term, up_term, wg, wu, sems, out_sem, *rest = scratch
         i = pl.program_id(0)
-        for first, x_ref, o_ref in ((0, g_ref, og_ref), (tiles, u_ref, ou_ref)):
-            last = first + tiles - 1
-
-            @pl.when(i == first)
-            def _(x_ref=x_ref):
-                acc[...] = nn(a_ref[...], x_ref[...])
-
-            @pl.when((i > first) & (i < last))
-            def _(x_ref=x_ref):
-                acc[...] += nn(a_ref[...], x_ref[...])
-
-            @pl.when(i == last)
-            def _(x_ref=x_ref, o_ref=o_ref):
-                o_ref[...] = (acc[...] + nn(a_ref[...], x_ref[...])).astype(BF16)
-
-    return scattering(
-        kernel, n, terms, ONE, identity,
-        grid=(2 * tiles,),
+        flows = [Scatter(n, down_term, down_out, *rest[:7]), Scatter(n, gate_term, gate_out, *rest[7:11])]
+        if last:
+            flows.append(Scatter(n, up_term, up_out, *rest[11:15]))
+        weights = [pltpu.make_async_copy(w.at[layer], v, sems.at[at]) for at, (w, v) in enumerate(((gw, wg), (uw, wu)))]
+
+        @pl.when(i == 0)
+        def _():
+            for c in weights:
+                c.start()
+            greet(n)
+
+        for step in sorted({p[0] for p in plan}):
+
+            @pl.when(i == step)
+            def _(step=step):
+                for when, action, which in plan:
+                    if when == step:
+                        getattr(flows[which], action)()
+
+        if not last:
+            out = pltpu.make_async_copy(up_term, up_out, out_sem.at[0])
+
+            @pl.when(i == low)
+            def _():
+                out.start()
+
+            @pl.when(i == steps - 1)
+            def _():
+                out.wait()
+
+        for first, x_ref, whole in ((0, dg_ref, gate_term), (middle, du_ref, up_term)):
+
+            @pl.when((i >= first) & (i < first + tiles))
+            def _(first=first, x_ref=x_ref, whole=whole):
+                @pl.when(i == first)
+                def _():
+                    acc[...] = jnp.zeros_like(acc)
+
+                acc[...] += nn(at_ref[...], x_ref[...])
+
+                @pl.when(i == first + tiles - 1)
+                def _():
+                    whole[...] = acc[...].astype(BF16)
+
+        @pl.when(i == low)
+        def _():
+            for c in weights:
+                c.wait()
+
+        @pl.when(i >= low)
+        def _():
+            @pl.loop(0, bt // inner)
+            def _(part):
+                rows = pl.ds(pl.multiple_of(part * inner, inner), inner)
+                da = (nt(dg_ref[rows, :], wg[...]) + nt(du_ref[rows, :], wu[...])).astype(BF16).astype(F32)
+                wide = h_ref[rows, :].astype(F32)
+                scale = scale_of(wide)
+                along = jnp.mean(da * wide, -1, keepdims=True)
+                dh = da * scale - wide * (scale * scale * scale * along)
+                o_ref[rows, :] = dy_ref[rows, :] + dh.astype(BF16)
+
+        if last:
+
+            @pl.when(i == steps - 1)
+            def _():
+                flows[2].end()
+
+    def late(i):
+        return (jnp.maximum(i - low, 0), 0)
+
+    def shard(rows, columns):
+        return pl.BlockSpec((rows // n, columns), lambda i: (0, 0), pipeline_mode=pl.Buffered(1))
+
+    scratch = [
+        pltpu.VMEM((d, f), F32),
+        pltpu.VMEM((d, f), BF16),
+        pltpu.VMEM((d, f), BF16),
+        pltpu.VMEM((d, f), BF16),
+        pltpu.VMEM((d, f), BF16),
+        pltpu.SemaphoreType.DMA((2,)),
+        pltpu.SemaphoreType.DMA((1,)),
+        *Scatter.scratch((f, d), n),
+        *Scatter.scratch((d, f), n, here=True),
+    ]
+    if last:
+        scratch += Scatter.scratch((d, f), n, here=True)
+    return pl.pallas_call(
+        kernel,
+        grid=(steps,),
         in_specs=[
-            pl.BlockSpec((d, bt), lambda i: (0, lax.rem(i, tiles))),
-            pl.BlockSpec((bt, f), lambda i: (jnp.minimum(i, tiles - 1), 0)),
-            pl.BlockSpec((bt, f), lambda i: (jnp.maximum(i - tiles, 0), 0)),
-        ],
-        out_specs=[pl.BlockSpec((d, f), lambda i: (0, 0))] * 2,
-        out_shape=[jax.ShapeDtypeStruct((d, f), BF16)] * 2,
-        scratch_shapes=[pltpu.VMEM((d, f), F32)],
-        name="weight_grads", flops=4 * t * d * f, nbytes=t * f * 4 + t * d * 4 + d * f * 4,
-    )(at, dg, du)
-
-
-def input_grad(n, terms, plan, identity, dg, du, h, dy, gate, up, layer, bm=256):
-    t, d = h.shape
-    f = dg.shape[1]
-
-    def kernel(dg_ref, du_ref, h_ref, dy_ref, gw, uw, o_ref, wg, wu, sems):
-        @pl.when(pl.program_id(0) == 0)
-        def _():
-            fetch(((gw.at[layer], wg), (uw.at[layer], wu)), sems)
-
-        da = (nt(dg_ref[...], wg[...]) + nt(du_ref[...], wu[...])).astype(BF16).astype(F32)
-        wide = h_ref[...].astype(F32)
-        scale = scale_of(wide)
-        along = jnp.mean(da * wide, -1, keepdims=True)
-        dh = da * scale - wide * (scale * scale * scale * along)
-        o_ref[...] = dy_ref[...] + dh.astype(BF16)
-
-    return scattering(
-        kernel, n, terms, plan, identity,
-        grid=(t // bm,),
-        in_specs=[rows_spec(bm, f), rows_spec(bm, f), rows_spec(bm, d), rows_spec(bm, d), ANY, ANY],
-        out_specs=[rows_spec(bm, d)],
-        out_shape=[jax.ShapeDtypeStruct((t, d), BF16)],
-        scratch_shapes=[pltpu.VMEM((d, f), BF16), pltpu.VMEM((d, f), BF16), pltpu.SemaphoreType.DMA((2,))],
-        name="input_grad", flops=4 * t * d * f, nbytes=t * f * 4 + t * d * 6,
-    )(dg, du, h, dy, gate, up)
+            pl.BlockSpec((d, bt), lambda i: (0, lax.rem(jnp.minimum(i, low - 1), tiles))),
+            pl.BlockSpec((bt, f), lambda i: (jnp.where(i < low, jnp.minimum(i, tiles - 1), i - low), 0)),
+            pl.BlockSpec((bt, f), lambda i: (jnp.where(i < low, jnp.maximum(i - middle, 0), i - low), 0)),
+            pl.BlockSpec((bt, d), late),
+            pl.BlockSpec((bt, d), late),
+            ANY,
+            ANY,
+            ANY,
+        ],
+        out_specs=[pl.BlockSpec((bt, d), late), shard(f, d), shard(d, f), shard(d, f) if last else ANY],
+        out_shape=[
+            jax.ShapeDtypeStruct((t, d), BF16),
+            jax.ShapeDtypeStruct((f // n, d), BF16),
+            jax.ShapeDtypeStruct((d // n, f), BF16),
+            jax.ShapeDtypeStruct((d // n if last else d, f), BF16),
+        ],
+        scratch_shapes=scratch,
+        compiler_params=pltpu.CompilerParams(
+            dimension_semantics=("arbitrary",),
+            vmem_limit_bytes=63 * 1024 * 1024,
+            collective_id=identity,
+            has_side_effects=True,
+        ),
+        cost_estimate=cost(8 * t * d * f, t * f * 8 + t * d * 10),
+        name="back",
+    )(at, dg, du, h, dy, gate, up, term)
 
 
 def solution(mesh):
@@ -642,11 +711,9 @@
         x, dy = (v.reshape(v.shape[-2:]) for v in (x, dy))
         at0, g0, u0, h1, gate, up, down = forward(x, w_gate, w_up, w_down, n)
         at1, dg1, du1, dwd1 = top_layer(h1, dy, gate, up, down, 1)
-        dwg1, dwu1, down1 = weight_grads(n, [dwd1], 1, at1, dg1, du1)
-        dh1, gate1 = input_grad(n, [dwg1], ONE, 2, dg1, du1, h1, dy, gate, up, 1)
-        dg0, du0, dwd0, up1 = low_layer(n, [dwu1], 3, g0, u0, dh1, down, 0)
-        dwg0, dwu0, down0 = weight_grads(n, [dwd0], 4, at0, dg0, du0)
-        dx, gate0, up0 = input_grad(n, [dwg0, dwu0], TWO, 5, dg0, du0, x, dh1, gate, up, 0)
+        dh1, down1, gate1, dwu1 = back(n, 1, dwd1, at1, dg1, du1, h1, dy, gate, up, 1, False)
+        dg0, du0, dwd0, up1 = low_layer(n, [dwu1], 2, g0, u0, dh1, down, 0)
+        dx, down0, gate0, up0 = back(n, 3, dwd0, at0, dg0, du0, x, dh1, gate, up, 0, True)
         return dx.reshape(shape), jnp.stack([gate0, gate1]), jnp.stack([up0, up1]), jnp.stack([down0, down1])
 
     seq, row = P(("rep", "dp")), P(None, "dp")

time: 536 us -> 505 us (0.942)
  Pallas kernels: 519 us -> 487 us
    pallas_call x5 -> x1, Pallas kernels: 285 us -> 61.2 us  [scattering(): pl.pallas_call(whole, grid=grid, in_specs=list(in_specs) + [ANY] * len(te...]
    pallas_call x0 -> x2, Pallas kernels: none -> 204 us  [back(): pl.pallas_call(kernel, grid=(steps,), in_specs=[pl.BlockSpec((d, bt), lam...]
    pallas_call x1, Pallas kernels: 140 us -> 128 us  [forward(): pl.pallas_call(kernel, grid=(steps,), in_specs=[pl.BlockSpec((bm, d), lam...]
where the time goes in v2:
time: 505 us; the launch traced here: 499 us
  Pallas kernels  487 us (96%)
  other arithmetic  7.85 us (2%)
    pallas_call x2, Pallas kernels, back(): pl.pallas_call(kernel, grid=(steps,), in_specs=[pl.BlockSpec((d, bt), lam...  204 us
    pallas_call x1, Pallas kernels, forward(): pl.pallas_call(kernel, grid=(steps,), in_specs=[pl.BlockSpec((bm, d), lam...  128 us
    pallas_call x1, Pallas kernels, top_layer(): pl.pallas_call(kernel, grid=(t // bm,), in_specs=[rows_spec(bm, d), rows_...  94.4 us
    pallas_call x1, Pallas kernels, scattering(): pl.pallas_call(whole, grid=grid, in_specs=list(in_specs) + [ANY] * len(te...  61.2 us

profile of v2, /device:TPU:112, one launch (start us, length us, event | category | flops | bytes accessed | tf_op | source)
XLA Modules:
  0.0 498.8 jit_solution(14543783921720655364)
XLA Ops:
  0.6 127.7 %forward.1 = (bf16[896,4096]{1,0:T(8,128)(2,1)}, f32[4096,2304]{1,0:T(8,128)}, f32[4096,2304]{1,0:T(8,128)}, bf16[4096,896]{1,0:T(8,128)(2,1)}, bf16[2,896,2304]...) custom-call(bf16[4096,896]{1,0:T(8,128)(2,1)} %bitcast.18, bf16[2,224,2304]{2,1,0:T(8,128)(2,1)} %gs.1, ...), custom_call_target="tpu_custom_call" | custom-call | flops 50734301184 | bytes 104857600 | tf_op jit(solution)/shard_map/forward/pallas_call | solution.py:265
  128.3 94.4 %top_layer.1 = (bf16[896,4096]{1,0:T(8,128)(2,1)}, bf16[4096,2304]{1,0:T(8,128)(2,1)}, bf16[4096,2304]{1,0:T(8,128)(2,1)}, bf16[2304,896]{1,0:T(8,128)(2,1)}) custom-call(bf16[4096,896]{1,0:T(8,128)(2,1)} %get-tuple-element.30.h_ref, bf16[4096,896]{1,0:T(8,128)(2,1)} %bitcast.16, bf16[2,896,2304]{2,1,0:T(8,128)(2,1)} %get-tuple-element.31.gw, ...), custom_call_target="tpu_custom_call" | custom-call | flops 67645734912 | bytes 59768832 | tf_op jit(solution)/shard_map/top_layer/pallas_call | solution.py:503
  222.7 97.7 %back.2 = (bf16[4096,896]{1,0:T(8,128)(2,1)}, bf16[576,896]{1,0:T(8,128)(2,1)}, bf16[224,2304]{1,0:T(8,128)(2,1)}, bf16[896,2304]{1,0:T(8,128)(2,1)}) custom-call(bf16[896,4096]{1,0:T(8,128)(2,1)} %get-tuple-element.34.at_ref, bf16[4096,2304]{1,0:T(8,128)(2,1)} %get-tuple-element.35.dg_ref, bf16[4096,2304]{1,0:T(8,128)(2,1)} %get-tuple-element.36.du_ref, ...), custom_call_target="tpu_custom_call" | custom-call | flops 67645734912 | bytes 112197632 | tf_op jit(solution)/shard_map/back/pallas_call | solution.py:674
  320.5 61.2 %low_layer.1 = (bf16[4096,2304]{1,0:T(8,128)(2,1)}, bf16[4096,2304]{1,0:T(8,128)(2,1)}, bf16[2304,896]{1,0:T(8,128)(2,1)}, bf16[224,2304]{1,0:T(8,128)(2,1)}) custom-call(f32[4096,2304]{1,0:T(8,128)} %get-tuple-element.28.refs_0_, f32[4096,2304]{1,0:T(8,128)} %get-tuple-element.29.refs_1_, bf16[4096,896]{1,0:T(8,128)(2,1)} %get-tuple-element.38.refs_2_.dy_ref, ...), custom_call_target="tpu_custom_call" | custom-call | flops 33822867456 | bytes 120586240 | tf_op jit(solution)/shard_map/low_layer/pallas_call | solution.py:442
  381.7 105.8 %back.3 = (bf16[4096,896]{1,0:T(8,128)(2,1)}, bf16[576,896]{1,0:T(8,128)(2,1)}, bf16[224,2304]{1,0:T(8,128)(2,1)}, bf16[224,2304]{1,0:T(8,128)(2,1)}) custom-call(bf16[896,4096]{1,0:T(8,128)(2,1)} %get-tuple-element.27.at_ref, bf16[4096,2304]{1,0:T(8,128)(2,1)} %get-tuple-element.40.dg_ref, bf16[4096,2304]{1,0:T(8,128)(2,1)} %get-tuple-element.41.du_ref, ...), custom_call_target="tpu_custom_call" | custom-call | flops 67645734912 | bytes 112197632 | tf_op jit(solution)/shard_map/back/pallas_call | solution.py:674
  487.5 0.0 copy-start
  487.5 4.8 pad_maximum_fusion
  492.3 3.1 pad_maximum_fusion.2
  495.3 0.0 copy-done
  495.3 3.0 copy.10
Async XLA Ops:
  487.5 7.9 %copy-start = (bf16[4096,896]{1,0:T(8,128)(2,1)S(1)}, bf16[4096,896]{1,0:T(8,128)(2,1)}, u32[]{:S(2)}) copy-start(bf16[4096,896]{1,0:T(8,128)(2,1)} %get-tuple-element.43) | copy-start | bytes 22020100

commit v3 on v2

--- a/solution.py
+++ b/solution.py
@@ -228,22 +228,24 @@
             flows[2 * pieces].arrived()
             fetch(((wd.at[0], vd),), local)
 
-        for p in range(pieces):
-
-            @pl.when(i // tiles == p)
-            def _(p=p):
-                wide = x_ref[...].astype(F32)
-                a = (wide * scale_of(wide)).astype(BF16)
-                if p == 0:
-                    at_ref[...] = a.T
-                rows = pl.ds(pl.multiple_of((i - p * tiles) * bm, bm), bm)
-                for c in chunks(width, cw):
-                    from_all = slice(p * width + c.start, p * width + c.stop)
-                    g = nn(a, vg[:, from_all])
-                    u = nn(a, vu[:, from_all])
-                    g_ref[:, c] = g
-                    u_ref[:, c] = u
-                    hidden[rows, from_all] = (g * sigmoid(g) * u).astype(BF16)
+        @pl.when(i < pieces * tiles)
+        def _():
+            p = i // tiles
+            wide = x_ref[...].astype(F32)
+            a = (wide * scale_of(wide)).astype(BF16)
+
+            @pl.when(i < tiles)
+            def _():
+                at_ref[...] = a.T
+
+            rows = pl.ds(pl.multiple_of((i - p * tiles) * bm, bm), bm)
+            for c in chunks(width, cw):
+                from_all = pl.ds(pl.multiple_of(p * width + c.start, 128), c.stop - c.start)
+                g = nn(a, vg[:, from_all])
+                u = nn(a, vu[:, from_all])
+                g_ref[:, c] = g
+                u_ref[:, c] = u
+                hidden[rows, from_all] = (g * sigmoid(g) * u).astype(BF16)
 
         @pl.when(i // tiles == pieces)
         def _():
@@ -466,15 +468,17 @@
 
 
 def finish_down(acc, o_ref, cw=256):
-    for c in chunks(acc.shape[1], cw):
+    @pl.loop(0, acc.shape[1] // cw)
+    def _(at):
+        c = pl.ds(pl.multiple_of(at * cw, cw), cw)
         o_ref[c, :] = acc[:, c].T.astype(BF16)
 
 
-def top_layer(h, dy, gate, up, down, layer, bm=512, cw=768):
+def top_layer(h, dy, gate, up, down, layer, bm=256, cw=2304):
     t, d = h.shape
     f = gate.shape[2]
 
-    def kernel(h_ref, dy_ref, gw, uw, dw, at_ref, dg_ref, du_ref, o_ref, wg, wu, wd, acc, sems):
+    def kernel(h_ref, dy_ref, gw, uw, dw, at_ref, both_ref, o_ref, wg, wu, wd, acc, sems):
         i = pl.program_id(0)
 
         @pl.when(i == 0)
@@ -492,8 +496,8 @@
             u = nn(a, wu[:, c])
             dh = nt(by, wd[c, :]).astype(BF16).astype(F32)
             dg, du, hidden = to_gates(g, u, dh)
-            dg_ref[:, c] = dg
-            du_ref[:, c] = du
+            both_ref[0, :, c] = dg
+            both_ref[1, :, c] = du
             acc[:, c] += nn(by_t, hidden)
 
         @pl.when(i == pl.num_programs(0) - 1)
@@ -506,14 +510,12 @@
         in_specs=[rows_spec(bm, d), rows_spec(bm, d)] + [ANY] * 3,
         out_specs=[
             pl.BlockSpec((d, bm), lambda i: (0, i)),
-            rows_spec(bm, f),
-            rows_spec(bm, f),
+            pl.BlockSpec((2, bm, f), lambda i: (0, i, 0)),
             pl.BlockSpec((f, d), lambda i: (0, 0)),
         ],
         out_shape=[
             jax.ShapeDtypeStruct((d, t), BF16),
-            jax.ShapeDtypeStruct((t, f), BF16),
-            jax.ShapeDtypeStruct((t, f), BF16),
+            jax.ShapeDtypeStruct((2, t, f), BF16),
             jax.ShapeDtypeStruct((f, d), BF16),
         ],
         scratch_shapes=[
@@ -533,7 +535,7 @@
     t, f = g.shape
     d = dy.shape[1]
 
-    def kernel(g_ref, u_ref, dy_ref, dw, dg_ref, du_ref, o_ref, wd, acc, sems):
+    def kernel(g_ref, u_ref, dy_ref, dw, both_ref, o_ref, wd, acc, sems):
         i = pl.program_id(0)
 
         @pl.when(i == 0)
@@ -546,8 +548,8 @@
         for c in chunks(f, cw):
             dh = nt(by, wd[c, :]).astype(BF16).astype(F32)
             dg, du, hidden = to_gates(g_ref[:, c], u_ref[:, c], dh)
-            dg_ref[:, c] = dg
-            du_ref[:, c] = du
+            both_ref[0, :, c] = dg
+            both_ref[1, :, c] = du
             acc[:, c] += nn(by_t, hidden)
 
         @pl.when(i == pl.num_programs(0) - 1)
@@ -558,10 +560,9 @@
         kernel, n, terms, ONE, identity,
         grid=(t // bm,),
         in_specs=[rows_spec(bm, f), rows_spec(bm, f), rows_spec(bm, d), ANY],
-        out_specs=[rows_spec(bm, f), rows_spec(bm, f), pl.BlockSpec((f, d), lambda i: (0, 0))],
+        out_specs=[pl.BlockSpec((2, bm, f), lambda i: (0, i, 0)), pl.BlockSpec((f, d), lambda i: (0, 0))],
         out_shape=[
-            jax.ShapeDtypeStruct((t, f), BF16),
-            jax.ShapeDtypeStruct((t, f), BF16),
+            jax.ShapeDtypeStruct((2, t, f), BF16),
             jax.ShapeDtypeStruct((f, d), BF16),
         ],
         scratch_shapes=[pltpu.VMEM((f, d), BF16), pltpu.VMEM((d, f), F32), pltpu.SemaphoreType.DMA((1,))],
@@ -569,9 +570,10 @@
     )(g, u, dy, down)
 
 
-def back(n, identity, term, at, dg, du, h, dy, gate, up, layer, last, bt=512, inner=256):
+def back(n, identity, term, at, both, h, dy, gate, up, layer, above=(), bt=512, inner=256):
     d, t = at.shape
-    f = dg.shape[1]
+    f = both.shape[2]
+    last = bool(above)
     tiles = t // bt
     steps = 3 * tiles
     middle, low = tiles, 2 * tiles
@@ -582,13 +584,16 @@
     if last:
         plan += [(low, "begin", 2), (low + 2, "neighbours", 2), (low + 4, "add", 2), (low + 5, "pass_on", 2)]
 
-    def kernel(at_ref, dg_ref, du_ref, h_ref, dy_ref, gw, uw, down_term, o_ref, down_out, gate_out, up_out, *scratch):
+    def kernel(at_ref, dg_ref, du_ref, h_ref, dy_ref, gw, uw, down_term, *refs):
+        others, (o_ref, *outs), scratch = refs[: len(above)], refs[len(above) : len(above) + 4], refs[len(above) + 4 :]
+        down_out, gate_out, up_out = (o.at[layer] for o in outs) if last else outs
         acc, gate_term, up_term, wg, wu, sems, out_sem, *rest = scratch
         i = pl.program_id(0)
         flows = [Scatter(n, down_term, down_out, *rest[:7]), Scatter(n, gate_term, gate_out, *rest[7:11])]
         if last:
             flows.append(Scatter(n, up_term, up_out, *rest[11:15]))
         weights = [pltpu.make_async_copy(w.at[layer], v, sems.at[at]) for at, (w, v) in enumerate(((gw, wg), (uw, wu)))]
+        weights += [pltpu.make_async_copy(o, outs[at].at[layer + 1], sems.at[2 + at]) for at, o in enumerate(others)]
 
         @pl.when(i == 0)
         def _():
@@ -615,19 +620,19 @@
             def _():
                 out.wait()
 
-        for first, x_ref, whole in ((0, dg_ref, gate_term), (middle, du_ref, up_term)):
-
-            @pl.when((i >= first) & (i < first + tiles))
-            def _(first=first, x_ref=x_ref, whole=whole):
-                @pl.when(i == first)
-                def _():
-                    acc[...] = jnp.zeros_like(acc)
-
-                acc[...] += nn(at_ref[...], x_ref[...])
-
-                @pl.when(i == first + tiles - 1)
-                def _():
-                    whole[...] = acc[...].astype(BF16)
+        @pl.when(i < low)
+        def _():
+            @pl.when(lax.rem(i, tiles) == 0)
+            def _():
+                acc[...] = jnp.zeros_like(acc)
+
+            acc[...] += nn(at_ref[...], dg_ref[...])
+
+        for step, whole in ((middle - 1, gate_term), (low - 1, up_term)):
+
+            @pl.when(i == step)
+            def _(whole=whole):
+                whole[...] = acc[...].astype(BF16)
 
         @pl.when(i == low)
         def _():
@@ -656,7 +661,11 @@
         return (jnp.maximum(i - low, 0), 0)
 
     def shard(rows, columns):
+        if last:
+            return pl.BlockSpec((2, rows // n, columns), lambda i: (0, 0, 0), pipeline_mode=pl.Buffered(1))
         return pl.BlockSpec((rows // n, columns), lambda i: (0, 0), pipeline_mode=pl.Buffered(1))
+
+    pair = (2,) if last else ()
 
     scratch = [
         pltpu.VMEM((d, f), F32),
@@ -664,7 +673,7 @@
         pltpu.VMEM((d, f), BF16),
         pltpu.VMEM((d, f), BF16),
         pltpu.VMEM((d, f), BF16),
-        pltpu.SemaphoreType.DMA((2,)),
+        pltpu.SemaphoreType.DMA((5,)),
         pltpu.SemaphoreType.DMA((1,)),
         *Scatter.scratch((f, d), n),
         *Scatter.scratch((d, f), n, here=True),
@@ -676,20 +685,24 @@
         grid=(steps,),
         in_specs=[
             pl.BlockSpec((d, bt), lambda i: (0, lax.rem(jnp.minimum(i, low - 1), tiles))),
-            pl.BlockSpec((bt, f), lambda i: (jnp.where(i < low, jnp.minimum(i, tiles - 1), i - low), 0)),
-            pl.BlockSpec((bt, f), lambda i: (jnp.where(i < low, jnp.maximum(i - middle, 0), i - low), 0)),
+            pl.BlockSpec(
+                (None, bt, f),
+                lambda i: (jnp.where(i < low, i // tiles, 0), jnp.where(i < low, lax.rem(i, tiles), i - low), 0),
+            ),
+            pl.BlockSpec((None, bt, f), lambda i: (1, jnp.maximum(i - low, 0), 0)),
             pl.BlockSpec((bt, d), late),
             pl.BlockSpec((bt, d), late),
             ANY,
             ANY,
             ANY,
+            *[ANY] * len(above),
         ],
         out_specs=[pl.BlockSpec((bt, d), late), shard(f, d), shard(d, f), shard(d, f) if last else ANY],
         out_shape=[
             jax.ShapeDtypeStruct((t, d), BF16),
-            jax.ShapeDtypeStruct((f // n, d), BF16),
-            jax.ShapeDtypeStruct((d // n, f), BF16),
-            jax.ShapeDtypeStruct((d // n if last else d, f), BF16),
+            jax.ShapeDtypeStruct((*pair, f // n, d), BF16),
+            jax.ShapeDtypeStruct((*pair, d // n, f), BF16),
+            jax.ShapeDtypeStruct((*pair, d // n if last else d, f), BF16),
         ],
         scratch_shapes=scratch,
         compiler_params=pltpu.CompilerParams(
@@ -700,7 +713,7 @@
         ),
         cost_estimate=cost(8 * t * d * f, t * f * 8 + t * d * 10),
         name="back",
-    )(at, dg, du, h, dy, gate, up, term)
+    )(at, both, both, h, dy, gate, up, term, *above)
 
 
 def solution(mesh):
@@ -710,11 +723,11 @@
         shape = x.shape
         x, dy = (v.reshape(v.shape[-2:]) for v in (x, dy))
         at0, g0, u0, h1, gate, up, down = forward(x, w_gate, w_up, w_down, n)
-        at1, dg1, du1, dwd1 = top_layer(h1, dy, gate, up, down, 1)
-        dh1, down1, gate1, dwu1 = back(n, 1, dwd1, at1, dg1, du1, h1, dy, gate, up, 1, False)
-        dg0, du0, dwd0, up1 = low_layer(n, [dwu1], 2, g0, u0, dh1, down, 0)
-        dx, down0, gate0, up0 = back(n, 3, dwd0, at0, dg0, du0, x, dh1, gate, up, 0, True)
-        return dx.reshape(shape), jnp.stack([gate0, gate1]), jnp.stack([up0, up1]), jnp.stack([down0, down1])
+        at1, both1, dwd1 = top_layer(h1, dy, gate, up, down, 1)
+        dh1, down1, gate1, dwu1 = back(n, 1, dwd1, at1, both1, h1, dy, gate, up, 1)
+        both0, dwd0, up1 = low_layer(n, [dwu1], 2, g0, u0, dh1, down, 0)
+        dx, downs, gates, ups = back(n, 3, dwd0, at0, both0, x, dh1, gate, up, 0, (down1, gate1, up1))
+        return dx.reshape(shape), gates, ups, downs
 
     seq, row = P(("rep", "dp")), P(None, "dp")
     out = P("rep", "dp")

time: 505 us -> 501 us (level); the launches traced: 499 us -> 500 us
  other arithmetic: 7.85 us -> 0 us
  local copies, waits for them, and re-layouts: 3.05 us -> 10.8 us
    another operation x2 -> x0, other arithmetic: 7.85 us -> none  [the longest x1 4.78 us: body(): jnp.stack([gate0, gate1])]
    unnamed x3 -> x10, local copies, waits for them, and re-layouts: 3.05 us -> 10.8 us
where the time goes in v3:
time: 501 us; the launch traced here: 500 us
  Pallas kernels  489 us (98%)
  local copies, waits for them, and re-layouts  10.8 us (2%)
    pallas_call x2, Pallas kernels, back(): pl.pallas_call(kernel, grid=(steps,), in_specs=[pl.BlockSpec((d, bt), lam...  205 us
    pallas_call x1, Pallas kernels, forward(): pl.pallas_call(kernel, grid=(steps,), in_specs=[pl.BlockSpec((bm, d), lam...  128 us
    pallas_call x1, Pallas kernels, top_layer(): pl.pallas_call(kernel, grid=(t // bm,), in_specs=[rows_spec(bm, d), rows_...  93.9 us
    pallas_call x1, Pallas kernels, scattering(): pl.pallas_call(whole, grid=grid, in_specs=list(in_specs) + [ANY] * len(te...  62 us
    unnamed x10, local copies, waits for them, and re-layouts  10.8 us

profile of v3, /device:TPU:112, one launch (start us, length us, event | category | flops | bytes accessed | tf_op | source)
XLA Modules:
  0.0 500.4 jit_solution(11083985937655029312)
XLA Ops:
  0.6 127.6 %forward.1 = (bf16[896,4096]{1,0:T(8,128)(2,1)}, f32[4096,2304]{1,0:T(8,128)}, f32[4096,2304]{1,0:T(8,128)}, bf16[4096,896]{1,0:T(8,128)(2,1)}, bf16[2,896,2304]...) custom-call(bf16[4096,896]{1,0:T(8,128)(2,1)} %bitcast.6, bf16[2,224,2304]{2,1,0:T(8,128)(2,1)} %gs.1, ...), custom_call_target="tpu_custom_call" | custom-call | flops 50734301184 | bytes 104857600 | tf_op jit(solution)/shard_map/forward/pallas_call | solution.py:267
  128.3 93.9 %top_layer.1 = (bf16[896,4096]{1,0:T(8,128)(2,1)}, bf16[2,4096,2304]{2,1,0:T(8,128)(2,1)}, bf16[2304,896]{1,0:T(8,128)(2,1)}) custom-call(bf16[4096,896]{1,0:T(8,128)(2,1)} %get-tuple-element.28.h_ref, bf16[4096,896]{1,0:T(8,128)(2,1)} %bitcast.4, bf16[2,896,2304]{2,1,0:T(8,128)(2,1)} %get-tuple-element.29.gw, bf16[2,896,2304]{2,1,0:T(8,128)(2,1)} %get-tuple-element.30.uw, ...), custom_call_target="tpu_custom_call" | custom-call | flops 67645734912 | bytes 59768832 | tf_op jit(solution)/shard_map/top_layer/pallas_call | solution.py:507
  222.2 97.9 %back.2 = (bf16[4096,896]{1,0:T(8,128)(2,1)}, bf16[576,896]{1,0:T(8,128)(2,1)}, bf16[224,2304]{1,0:T(8,128)(2,1)}, bf16[896,2304]{1,0:T(8,128)(2,1)}) custom-call(bf16[896,4096]{1,0:T(8,128)(2,1)} %get-tuple-element.32.at_ref, bf16[2,4096,2304]{2,1,0:T(8,128)(2,1)} %get-tuple-element.33.dg_ref.du_ref, ...), custom_call_target="tpu_custom_call" | custom-call | flops 67645734912 | bytes 112197632 | tf_op jit(solution)/shard_map/back/pallas_call | solution.py:683
  320.2 62.0 %low_layer.1 = (bf16[2,4096,2304]{2,1,0:T(8,128)(2,1)}, bf16[2304,896]{1,0:T(8,128)(2,1)}, bf16[224,2304]{1,0:T(8,128)(2,1)}) custom-call(f32[4096,2304]{1,0:T(8,128)} %get-tuple-element.26.refs_0_, f32[4096,2304]{1,0:T(8,128)} %get-tuple-element.27.refs_1_, bf16[4096,896]{1,0:T(8,128)(2,1)} %get-tuple-element.35.refs_2_.dy_ref, ...), custom_call_target="tpu_custom_call" | custom-call | flops 33822867456 | bytes 120586240 | tf_op jit(solution)/shard_map/low_layer/pallas_call | solution.py:444
  382.1 107.4 %back.3 = (bf16[4096,896]{1,0:T(8,128)(2,1)}, bf16[2,576,896]{2,1,0:T(8,128)(2,1)}, bf16[2,224,2304]{2,1,0:T(8,128)(2,1)}, bf16[2,224,2304]{2,1,0:T(8,128)(2,1)}) custom-call(bf16[896,4096]{1,0:T(8,128)(2,1)} %get-tuple-element.25.at_ref, bf16[2,4096,2304]{2,1,0:T(8,128)(2,1)} %get-tuple-element.37.dg_ref.du_ref, ...), custom_call_target="tpu_custom_call" | custom-call | flops 67645734912 | bytes 112197632 | tf_op jit(solution)/shard_map/back/pallas_call | solution.py:683
  489.6 0.0 copy-start.2
  489.6 0.0 copy-start.1
  489.6 6.9 %copy.13 = bf16[1,4096,896]{2,1,0:T(8,128)(2,1)} copy(bf16[1,4096,896]{2,1,0:T(8,128)(2,1)} %bitcast.3) | data formatting | bytes 14680064
  496.4 0.0 copy-done.2
  496.4 0.0 copy-start
  496.4 1.3 copy.14
  497.7 0.0 copy-done.1
  497.8 1.3 copy.15
  499.1 0.0 copy-done
  499.1 1.3 copy.16
Async XLA Ops:
  489.6 6.9 %copy-start.2 = (bf16[2,224,2304]{2,1,0:T(8,128)(2,1)S(1)}, bf16[2,224,2304]{2,1,0:T(8,128)(2,1)}, u32[]{:S(2)}) copy-start(bf16[2,224,2304]{2,1,0:T(8,128)(2,1)} %get-tuple-element.51) | copy-start | bytes 6193156
  489.6 8.2 %copy-start.1 = (bf16[2,224,2304]{2,1,0:T(8,128)(2,1)S(1)}, bf16[2,224,2304]{2,1,0:T(8,128)(2,1)}, u32[]{:S(2)}) copy-start(bf16[2,224,2304]{2,1,0:T(8,128)(2,1)} %get-tuple-element.52) | copy-start | bytes 6193156
  496.4 2.6 copy-start

commit v4 on v3

--- a/solution.py
+++ b/solution.py
@@ -132,7 +132,7 @@
         units.append((2, layer, whole_d, by_rows))
     count = len(units)
 
-    sizes = [(u[2].stop - u[2].start) * halves[0 if u[0] < 2 else 1] * 2 / 60e3 for u in units]
+    sizes = [(u[2].stop - u[2].start) * halves[0 if u[0] < 2 else 1] * 2 / 53e3 for u in units]
     order = [("s", 0), ("s", 1), ("f", 0), ("f", 1), ("s", 2), ("s", 3)]
     for k in range(2, count):
         order.append(("f", k))
@@ -716,6 +716,23 @@
     )(at, both, both, h, dy, gate, up, term, *above)
 
 
+def handed_on(x, bm=512):
+    def kernel(x_ref, o_ref):
+        o_ref[...] = x_ref[...]
+
+    t, d = x.shape
+    return pl.pallas_call(
+        kernel,
+        grid=(t // bm,),
+        in_specs=[rows_spec(bm, d)],
+        out_specs=rows_spec(bm, d),
+        out_shape=jax.ShapeDtypeStruct((t, d), BF16),
+        compiler_params=params(),
+        cost_estimate=cost(0, t * d * 4),
+        name="handed_on",
+    )(x)
+
+
 def solution(mesh):
     n = mesh.shape["dp"]
 
@@ -727,7 +744,7 @@
         dh1, down1, gate1, dwu1 = back(n, 1, dwd1, at1, both1, h1, dy, gate, up, 1)
         both0, dwd0, up1 = low_layer(n, [dwu1], 2, g0, u0, dh1, down, 0)
         dx, downs, gates, ups = back(n, 3, dwd0, at0, both0, x, dh1, gate, up, 0, (down1, gate1, up1))
-        return dx.reshape(shape), gates, ups, downs
+        return handed_on(dx).reshape(shape), gates, ups, downs
 
     seq, row = P(("rep", "dp")), P(None, "dp")
     out = P("rep", "dp")

time: 501 us -> 499 us (level)
  local copies, waits for them, and re-layouts: 10.8 us -> 3.92 us
    pallas_call x0 -> x1, Pallas kernels: none -> 8.88 us  [handed_on(): pl.pallas_call(kernel, grid=(t // bm,), in_specs=[rows_spec(bm, d)], out_...]
    unnamed x10 -> x9, local copies, waits for them, and re-layouts: 10.8 us -> 3.92 us
    pallas_call x1, Pallas kernels: 128 us -> 122 us  [forward(): pl.pallas_call(kernel, grid=(steps,), in_specs=[pl.BlockSpec((bm, d), lam...]
where the time goes in v4:
time: 499 us
  Pallas kernels  494 us (99%)
    pallas_call x2, Pallas kernels, back(): pl.pallas_call(kernel, grid=(steps,), in_specs=[pl.BlockSpec((d, bt), lam...  209 us
    pallas_call x1, Pallas kernels, forward(): pl.pallas_call(kernel, grid=(steps,), in_specs=[pl.BlockSpec((bm, d), lam...  122 us
    pallas_call x1, Pallas kernels, top_layer(): pl.pallas_call(kernel, grid=(t // bm,), in_specs=[rows_spec(bm, d), rows_...  93.9 us
    pallas_call x1, Pallas kernels, scattering(): pl.pallas_call(whole, grid=grid, in_specs=list(in_specs) + [ANY] * len(te...  61.1 us

profile of v4, /device:TPU:112, one launch (start us, length us, event | category | flops | bytes accessed | tf_op | source)
XLA Modules:
  0.0 499.1 jit_solution(10660304432204511808)
XLA Ops:
  0.6 122.0 %forward.1 = (bf16[896,4096]{1,0:T(8,128)(2,1)}, f32[4096,2304]{1,0:T(8,128)}, f32[4096,2304]{1,0:T(8,128)}, bf16[4096,896]{1,0:T(8,128)(2,1)}, bf16[2,896,2304]...) custom-call(bf16[4096,896]{1,0:T(8,128)(2,1)} %bitcast.6, bf16[2,224,2304]{2,1,0:T(8,128)(2,1)} %gs.1, ...), custom_call_target="tpu_custom_call" | custom-call | flops 50734301184 | bytes 104857600 | tf_op jit(solution)/shard_map/forward/pallas_call | solution.py:267
  122.6 93.9 %top_layer.1 = (bf16[896,4096]{1,0:T(8,128)(2,1)}, bf16[2,4096,2304]{2,1,0:T(8,128)(2,1)}, bf16[2304,896]{1,0:T(8,128)(2,1)}) custom-call(bf16[4096,896]{1,0:T(8,128)(2,1)} %get-tuple-element.28.h_ref, bf16[4096,896]{1,0:T(8,128)(2,1)} %bitcast.4, bf16[2,896,2304]{2,1,0:T(8,128)(2,1)} %get-tuple-element.29.gw, bf16[2,896,2304]{2,1,0:T(8,128)(2,1)} %get-tuple-element.30.uw, ...), custom_call_target="tpu_custom_call" | custom-call | flops 67645734912 | bytes 59768832 | tf_op jit(solution)/shard_map/top_layer/pallas_call | solution.py:507
  216.6 97.4 %back.2 = (bf16[4096,896]{1,0:T(8,128)(2,1)}, bf16[576,896]{1,0:T(8,128)(2,1)}, bf16[224,2304]{1,0:T(8,128)(2,1)}, bf16[896,2304]{1,0:T(8,128)(2,1)}) custom-call(bf16[896,4096]{1,0:T(8,128)(2,1)} %get-tuple-element.32.at_ref, bf16[2,4096,2304]{2,1,0:T(8,128)(2,1)} %get-tuple-element.33.dg_ref.du_ref, ...), custom_call_target="tpu_custom_call" | custom-call | flops 67645734912 | bytes 112197632 | tf_op jit(solution)/shard_map/back/pallas_call | solution.py:683
  314.0 61.1 %low_layer.1 = (bf16[2,4096,2304]{2,1,0:T(8,128)(2,1)}, bf16[2304,896]{1,0:T(8,128)(2,1)}, bf16[224,2304]{1,0:T(8,128)(2,1)}) custom-call(f32[4096,2304]{1,0:T(8,128)} %get-tuple-element.26.refs_0_, f32[4096,2304]{1,0:T(8,128)} %get-tuple-element.27.refs_1_, bf16[4096,896]{1,0:T(8,128)(2,1)} %get-tuple-element.35.refs_2_.dy_ref, ...), custom_call_target="tpu_custom_call" | custom-call | flops 33822867456 | bytes 120586240 | tf_op jit(solution)/shard_map/low_layer/pallas_call | solution.py:444
  375.1 111.2 %back.3 = (bf16[4096,896]{1,0:T(8,128)(2,1)}, bf16[2,576,896]{2,1,0:T(8,128)(2,1)}, bf16[2,224,2304]{2,1,0:T(8,128)(2,1)}, bf16[2,224,2304]{2,1,0:T(8,128)(2,1)}) custom-call(bf16[896,4096]{1,0:T(8,128)(2,1)} %get-tuple-element.25.at_ref, bf16[2,4096,2304]{2,1,0:T(8,128)(2,1)} %get-tuple-element.37.dg_ref.du_ref, ...), custom_call_target="tpu_custom_call" | custom-call | flops 67645734912 | bytes 112197632 | tf_op jit(solution)/shard_map/back/pallas_call | solution.py:683
  486.3 0.0 copy-start.2
  486.3 0.0 copy-start.1
  486.3 8.9 %handed_on.1 = bf16[4096,896]{1,0:T(8,128)(2,1)} custom-call(bf16[4096,896]{1,0:T(8,128)(2,1)} %get-tuple-element.42.x_ref), custom_call_target="tpu_custom_call" | custom-call | bytes 14680064 | tf_op jit(solution)/shard_map/handed_on/pallas_call | solution.py:724
  495.2 0.0 copy-start
  495.2 0.0 copy-done.2
  495.2 1.3 copy.12
  496.5 0.0 copy-done.1
  496.5 1.3 copy.13
  497.8 0.0 copy-done
  497.8 1.3 copy.14
Async XLA Ops:
  486.3 8.9 %copy-start.2 = (bf16[2,224,2304]{2,1,0:T(8,128)(2,1)S(1)}, bf16[2,224,2304]{2,1,0:T(8,128)(2,1)}, u32[]{:S(2)}) copy-start(bf16[2,224,2304]{2,1,0:T(8,128)(2,1)} %get-tuple-element.51) | copy-start | bytes 6193156
  486.3 10.2 %copy-start.1 = (bf16[2,224,2304]{2,1,0:T(8,128)(2,1)S(1)}, bf16[2,224,2304]{2,1,0:T(8,128)(2,1)}, u32[]{:S(2)}) copy-start(bf16[2,224,2304]{2,1,0:T(8,128)(2,1)} %get-tuple-element.52) | copy-start | bytes 6193156
  495.2 2.6 copy-start
